TPU v7x, 32 devices: a whole 2x2x4 slice. The times are simulated.
32 devices in a mesh: row: 4 (over y, x), col: 8 (over z, core).
Axes of the slice: x: 2, y: 2, z: 4, core: 2. Of those that a mesh axis runs over, the one named last changes fastest.
Arguments:
- tokens: bfloat16 [4096, 2048], P(('row', 'col')), may hold values from -6 to 6
- expert_ids: int32 [4096, 8], P(('row', 'col')), may hold values from 0 to 31, all different within a row; in each aligned block of 128 rows (0 to 127, 128 to 255, ...) at most 40 rows name the same one
- gate_probs: float32 [4096, 8], P(('row', 'col')), may hold values from 0.05 to 0.5
- w_gate: bfloat16 [32, 2048, 768], P(('row', 'col')), may hold values from -0.125 to 0.125
- w_up: bfloat16 [32, 2048, 768], P(('row', 'col')), may hold values from -0.125 to 0.125
- w_down: bfloat16 [32, 768, 2048], P(('row', 'col')), may hold values from -0.21875 to 0.21875
Outputs:
- mixed: bfloat16 [4096, 2048], P(('row', 'col'))
Inputs may be any that keep to these rules, and one draw needn't show every extreme that they name: `expert_ids`: each row names 8 different experts; among the rows of one device (aligned blocks of 128 rows) no expert is named more than 40 times.
All inputs are finite; a program needn't handle non-finite values.
Results may differ from a plain program's by a relative error of at most 0.0058.
Values may be sent and summed in bfloat16 or wider, within the bound.
A program may use at most 128 MiB of HBM per device.

v0:
```python
import functools
import math

import jax
import jax.numpy as jnp
from jax import lax
from jax.experimental import pallas as pl
from jax.experimental.pallas import tpu as pltpu
from jax.sharding import PartitionSpec as P

MESH = pl.DeviceIdType.MESH
BF16 = jnp.bfloat16
F32 = jnp.float32
PIECES = 2


def moe_kernel(
    rows, cols, slots, group, pieces,
    ids_in, probs_in, tok_in, wg_in, wu_in, wd_in, out_ref,
    ids_all, probs_all, tok, wg, wu, wd, disp, comb, hid, xs, xr, yr, pr, acc, zs, zr,
    load_sem, ids_send, ids_recv, probs_send, probs_recv, ztok_send, ztok_recv, ctok_send, ctok_recv,
    x_send, x_recv, y_send, y_recv, p_send, p_recv, z_send, z_recv,
):
    r = lax.axis_index("row")
    c = lax.axis_index("col")
    chips = cols // 2
    chip, core = c // 2, c % 2
    mate = 2 * chip + (1 - core)
    count, width = tok_in.shape
    per = group // 2
    chunks = chips // per
    part = group * slots
    total = rows * part
    hidden = wg.shape[1]
    f_tile = math.gcd(hidden, 256)
    d_tile = math.gcd(width // pieces, 512)
    piece = width // pieces

    def remote(src, dst, send, recv, row, col):
        return pltpu.make_async_remote_copy(
            src_ref=src, dst_ref=dst, send_sem=send, recv_sem=recv,
            device_id=(row, col), device_id_type=MESH,
        )

    short = jnp.minimum(chip, chips - 1 - chip)
    side = jnp.where(2 * chip < chips, 1, -1)
    order, signs = [chip], [None]
    for p in range(1, chips):
        both = p <= 2 * short
        sign = jnp.where(both, 1 if p % 2 else -1, side)
        far = jnp.where(both, (p + 1) // 2, p - short)
        order.append(chip + sign * far)
        signs.append(sign)

    load_tok = pltpu.make_async_copy(tok_in, tok.at[chip, 0], load_sem.at[0])
    load_ids = pltpu.make_async_copy(ids_in, ids_all.at[chip, 0], load_sem.at[1])
    load_probs = pltpu.make_async_copy(probs_in, probs_all.at[chip, 0], load_sem.at[5])
    load_w = [
        pltpu.make_async_copy(wg_in.at[0], wg, load_sem.at[2]),
        pltpu.make_async_copy(wu_in.at[0], wu, load_sem.at[3]),
        pltpu.make_async_copy(wd_in.at[0], wd, load_sem.at[4]),
    ]
    load_tok.start()
    load_ids.start()
    load_probs.start()

    barrier = pltpu.get_barrier_semaphore()
    for d in range(1, cols):
        pl.semaphore_signal(barrier, inc=1, device_id=(r, (c + d) % cols), device_id_type=MESH)
    for j in range(1, rows):
        pl.semaphore_signal(barrier, inc=1, device_id=((r + j) % rows, c), device_id_type=MESH)
    pl.semaphore_wait(barrier, cols - 1 + rows - 1)

    def hop(q, send, to):
        return remote(
            tok.at[q, 0], tok.at[q, 0], ztok_send.at[send], ztok_recv.at[q],
            r, 2 * ((to + chips) % chips) + core,
        )

    def onward(p, act):
        if p == 0:
            @pl.when(chip > 0)
            def _():
                act(hop(chip, 0, chip - 1))

            @pl.when(chip < chips - 1)
            def _():
                act(hop(chip, chips, chip + 1))
        else:
            to = chip - signs[p]

            @pl.when((to >= 0) & (to < chips))
            def _():
                act(hop(order[p], p, to))

    ctok = [
        remote(tok.at[q, 0], tok.at[q, 1], ctok_send.at[p], ctok_recv.at[p], r, mate)
        for p, q in enumerate(order)
    ]
    load_tok.wait()
    ctok[0].start()
    load_ids.wait()
    load_probs.wait()

    def routing(d, t, slot):
        far, other = d // 2, d % 2
        to = 2 * t + (core if other == 0 else 1 - core)
        return (
            remote(
                ids_all.at[chip, 0], ids_all.at[slot, other],
                ids_send.at[d], ids_recv.at[slot, other], r, to,
            ),
            remote(
                probs_all.at[chip, 0], probs_all.at[slot, other],
                probs_send.at[d], probs_recv.at[slot, other], r, to,
            ),
        )

    for d in range(1, cols):
        for copy in routing(d, (chip + d // 2) % chips, chip):
            copy.start()
    onward(0, lambda copy: copy.start())
    for copy in load_w:
        copy.start()
    earlier = (
        lax.broadcasted_iota(jnp.int32, (count, count), 0)
        < lax.broadcasted_iota(jnp.int32, (count, count), 1)
    ).astype(BF16)
    slot_of = lax.broadcasted_iota(jnp.int32, (part, count), 0).astype(F32)
    lane_rows = 16
    row_id = lax.broadcasted_iota(jnp.int32, (lane_rows, count), 0)

    def route(i):
        for s in range(group):
            ids = ids_all[order[i * per + s // 2], s % 2]
            probs = probs_all[order[i * per + s // 2], s % 2]
            named = jnp.zeros((lane_rows, count), F32)
            weights = []
            for j in range(rows):
                expert = ((r + j) % rows) * cols + c
                hit = (ids == expert).astype(F32)
                named = jnp.where(row_id == j, jnp.sum(hit, axis=0, keepdims=True), named)
                weights.append(jnp.sum(hit * probs, axis=0, keepdims=True))
            rank = jnp.dot(named.astype(BF16), earlier, preferred_element_type=F32)
            key = jnp.where(named > 0.5, rank + float(s * slots), -1.0)
            for j in range(rows):
                one = (slot_of == key[j:j + 1, :]).astype(F32)
                disp[j * part:(j + 1) * part, s * count:(s + 1) * count] = one.astype(BF16)
                comb[i, j * part:(j + 1) * part, s * count:(s + 1) * count] = (
                    one * weights[j]
                ).astype(BF16)

    x_out, y_out, p_out, z_out = {}, {}, {}, {}

    def dispatch(i):
        for d in range(i * per, (i + 1) * per):
            if d > 0:
                hop(order[d], d, chip).wait_recv()
                onward(d, lambda copy: copy.start())
                ctok[d].start()
            for other in range(0 if d > 0 else 1, 2):
                for copy in routing(other, order[d], order[d]):
                    copy.wait_recv()
        route(i)
        for d in range(i * per, (i + 1) * per):
            ctok[d].wait_recv()

        def tile(n, _):
            at = pl.ds(pl.multiple_of(n * d_tile, d_tile), d_tile)
            block = jnp.concatenate(
                [tok[q, :, :, at].reshape(2 * count, d_tile) for q in order[i * per:(i + 1) * per]]
            )
            res = jnp.dot(disp[...], block, preferred_element_type=F32).astype(BF16)
            xr[i, 0, :, at] = res[:part]
            xs[i, :, :, at] = res[part:].reshape(rows - 1, part, d_tile)
            return 0

        lax.fori_loop(0, width // d_tile, tile, 0)
        for j in range(1, rows):
            copy = remote(
                xs.at[i, j - 1], xr.at[i, j], x_send.at[i, j], x_recv.at[i, j],
                (r + j) % rows, c,
            )
            copy.start()
            x_out[i, j] = copy

    def experts(i, first):
        for j in range(1, rows):
            x_out[i, j].wait()
        if first:
            for copy in load_w:
                copy.wait()

        def up_tile(n, _):
            at = pl.ds(pl.multiple_of(n * f_tile, f_tile), f_tile)
            x = xr[i].reshape(total, width)
            gate = jnp.dot(x, wg[:, at], preferred_element_type=F32)
            up = jnp.dot(x, wu[:, at], preferred_element_type=F32)
            hid[:, at] = (gate / (1.0 + jnp.exp(-gate)) * up).astype(BF16)
            return 0

        lax.fori_loop(0, hidden // f_tile, up_tile, 0)

        def down_tile(n, _):
            at = pl.ds(pl.multiple_of(n * d_tile, d_tile), d_tile)
            res = jnp.dot(hid[...], wd[:, at], preferred_element_type=F32).astype(BF16)
            yr[i, 0, :, at] = res[:part]
            xs[i, :, :, at] = res[part:].reshape(rows - 1, part, d_tile)
            return 0

        for h in range(pieces):
            at = pl.ds(h * piece, piece)
            lax.fori_loop(h * piece // d_tile, (h + 1) * piece // d_tile, down_tile, 0)
            for j in range(1, rows):
                copy = remote(
                    xs.at[i, j - 1, :, at], yr.at[i, j, :, at],
                    y_send.at[i, j, h], y_recv.at[i, j, h], (r + rows - j) % rows, c,
                )
                copy.start()
                y_out[i, j, h] = copy

    def combine(i, h):
        for j in range(1, rows):
            y_out[i, j, h].wait()

        def tile(n, _):
            at = pl.ds(pl.multiple_of(n * d_tile, d_tile), d_tile)
            y = yr[i, :, :, at].reshape(total, d_tile)
            res = lax.dot_general(
                comb[i], y, (((0,), (0,)), ((), ())), preferred_element_type=F32
            )
            for p in range(per):
                d = i * per + p
                acc[d, :, at] = res[2 * p * count:(2 * p + 1) * count]
                tok[order[d], 1, :, at] = res[(2 * p + 1) * count:(2 * p + 2) * count].astype(BF16)
            return 0

        lax.fori_loop(h * piece // d_tile, (h + 1) * piece // d_tile, tile, 0)
        at = pl.ds(h * piece, piece)
        for d in range(i * per, (i + 1) * per):
            copy = remote(
                tok.at[order[d], 1, :, at], pr.at[d, :, at], p_send.at[d, h], p_recv.at[d, h],
                r, mate,
            )
            copy.start()
            p_out[d, h] = copy

    def partial_copy(d, h, slot):
        at = pl.ds(h * piece, piece)
        return remote(
            zs.at[d - 1, :, at], zr.at[slot, :, at], z_send.at[d, h], z_recv.at[slot, h],
            r, 2 * order[d] + core,
        )

    def reduce_cores(i, h):
        at = pl.ds(h * piece, piece)
        for d in range(i * per, (i + 1) * per):
            p_out[d, h].wait()
            if d > 0:
                zs[d - 1, :, at] = (acc[d, :, at] + pr[d, :, at].astype(F32)).astype(BF16)
                partial_copy(d, h, chip).start()

    turn = list(range(chunks // 2, chunks)) + list(range(chunks // 2 - 1, -1, -1))
    for i in range(chunks):
        dispatch(i)
    for n in range(chunks):
        experts(turn[n], n == 0)
    for n in range(chunks):
        for h in range(pieces):
            combine(turn[n], h)
            reduce_cores(turn[n], h)
    for h in range(pieces):
        at = pl.ds(h * piece, piece)
        result = acc[0, :, at] + pr[0, :, at].astype(F32)
        for d in range(1, chips):
            partial_copy(d, h, order[d]).wait()
            result = result + zr[order[d], :, at].astype(F32)
        out_ref[:, at] = result.astype(BF16)
    for d in range(1, cols):
        for copy in routing(d, (chip + d // 2) % chips, chip):
            copy.wait_send()
    for d in range(chips):
        onward(d, lambda copy: copy.wait_send())
        ctok[d].wait_send()


def body(tokens, expert_ids, gate_probs, w_gate, w_up, w_down):
    count, choices = expert_ids.shape
    width = tokens.shape[1]
    hidden = w_gate.shape[2]
    rows = lax.axis_size("row")
    cols = lax.axis_size("col")
    slots = 5 * count * choices // (4 * rows * cols * w_gate.shape[0])
    group = 2
    while group * slots % 16:
        group *= 2
    chips = cols // 2
    chunks = cols // group
    part = group * slots
    any_spec = pl.BlockSpec(memory_space=pl.ANY)
    dma = pltpu.SemaphoreType.DMA
    scratch = [
        pltpu.VMEM((chips, 2, choices, count), jnp.int32),
        pltpu.VMEM((chips, 2, choices, count), F32),
        pltpu.VMEM((chips, 2, count, width), BF16),
        pltpu.VMEM((width, hidden), BF16),
        pltpu.VMEM((width, hidden), BF16),
        pltpu.VMEM((hidden, width), BF16),
        pltpu.VMEM((rows * part, group * count), BF16),
        pltpu.VMEM((chunks, rows * part, group * count), BF16),
        pltpu.VMEM((rows * part, hidden), BF16),
        pltpu.VMEM((chunks, rows - 1, part, width), BF16),
        pltpu.VMEM((chunks, rows, part, width), BF16),
        pltpu.VMEM((chunks, rows, part, width), BF16),
        pltpu.VMEM((chips, count, width), BF16),
        pltpu.VMEM((chips, count, width), F32),
        pltpu.VMEM((chips - 1, count, width), BF16),
        pltpu.VMEM((chips, count, width), BF16),
        dma((6,)),
        dma((cols,)), dma((chips, 2)),
        dma((cols,)), dma((chips, 2)),
        dma((chips + 1,)), dma((chips,)),
        dma((chips,)), dma((chips,)),
        dma((chunks, rows)), dma((chunks, rows)),
        dma((chunks, rows, PIECES)), dma((chunks, rows, PIECES)),
        dma((chips, PIECES)), dma((chips, PIECES)),
        dma((chips, PIECES)), dma((chips, PIECES)),
    ]
    return pl.pallas_call(
        functools.partial(moe_kernel, rows, cols, slots, group, PIECES),
        out_shape=jax.ShapeDtypeStruct((count, width), BF16),
        in_specs=[any_spec] * 6,
        out_specs=pl.BlockSpec(memory_space=pltpu.VMEM),
        scratch_shapes=scratch,
        compiler_params=pltpu.CompilerParams(
            collective_id=0, has_side_effects=True, vmem_limit_bytes=67043328
        ),
    )(expert_ids.T, gate_probs.T, tokens, w_gate, w_up, w_down)


def solution(mesh):
    in_specs = (
        P(("row", "col"), None),
        P(("row", "col"), None),
        P(("row", "col"), None),
        P(("row", "col"), None, None),
        P(("row", "col"), None, None),
        P(("row", "col"), None, None),
    )
    out_specs = P(("row", "col"), None)
    return jax.shard_map(body, mesh=mesh, in_specs=in_specs, out_specs=out_specs, check_vma=False)
```

profile of v0, /device:TPU:0, one launch (start us, length us, event | category | flops | bytes accessed | tf_op | source)
XLA Modules:
  0.0 133.1 jit_solution(15483702862499729273)
XLA Ops:
  0.0 131.2 %shard_map.64 = bf16[128,2048]{1,0:T(8,128)(2,1)} custom-call(s32[8,128]{1,0:T(8,128)} %bitcast.2, f32[8,128]{1,0:T(8,128)} %bitcast.3, bf16[128,2048]{1,0:T(8,128)(2,1)} %tok_in.1, bf16[1,2048,768]{2,1,0:T(8,128)(2,1)} %wg_in.1, bf16[1,2048,768]{2,1,0:T(8,128)(2,1)} %wu_in.1, bf16[1,768,2048]{2,1,0:T(8,128)(2,1)} %wd_in.1), custom_call_target="tpu_custom_call" | custom-call | tf_op jit(solution)/shard_map/pallas_call | solution.py:329
  131.2 1.9 %copy.8 = bf16[128,2048]{1,0:T(8,128)(2,1)} copy(bf16[128,2048]{1,0:T(8,128)(2,1)} %shard_map.64) | data formatting | bytes 1048576
where the time goes:
time: 133 us
  Pallas kernels  131 us (98%)
  local copies, waits for them, and re-layouts  1.88 us (1%)
    pallas_call x1, Pallas kernels, body(): pl.pallas_call(functools.partial(moe_kernel, rows, cols, slots, group, PI...  131 us

commit v1 on v0

v1 whole, which is shorter than its diff:
```python
import functools
import math

import jax
import jax.numpy as jnp
from jax import lax
from jax.experimental import pallas as pl
from jax.experimental.pallas import tpu as pltpu
from jax.sharding import PartitionSpec as P

MESH = pl.DeviceIdType.MESH
BF16 = jnp.bfloat16
F32 = jnp.float32
PIECES = 2
OWN, PAR = 0, 1


def flip(r, j):
    out, bit = r, 1
    while bit <= j:
        if j & bit:
            out = out + bit * (1 - 2 * ((r // bit) % 2))
        bit *= 2
    return out


def plan(chunks, per, chips):
    hops = range(1, chips)
    if per > 1 or chunks < 4:
        every = range(chunks)
        return (
            [("D", i) for i in every] + [("F", d, "all") for d in range(chips)]
            + [("P", i) for i in every] + [("X", i, 1) for i in every]
            + [("C", o, i) for o in (OWN, PAR) for i in every]
            + [("R", o, k) for o in (OWN, PAR) for k in hops] + [("H", PAR), ("H", OWN)]
        )
    last = chunks - 1
    seq = [("D", 0), ("D", 1), ("F", 0, "all"), ("P", 0), ("X", 0, 1)]
    for i in range(2, chunks):
        seq += [("D", i), ("X", i - 1, 0)]
        if i == 2:
            seq += [("C", OWN, 0), ("C", PAR, 0)]
        else:
            seq += [("C", OWN, i - 2), ("R", OWN, i - 2)]
    seq += [("F", d, "mid") for d in range(1, last)]
    seq += [("X", last, 0), ("C", OWN, last - 1), ("R", OWN, last - 1), ("F", last, "mid")]
    for i in hops:
        seq += [("F", i, "end"), ("P", i), ("X", i, 2)]
        if i == 1:
            seq += [("C", OWN, last), ("R", OWN, last)]
        seq += [("C", PAR, i), ("R", PAR, i)]
    return seq + [("H", PAR), ("H", OWN)]


def moe_kernel(
    rows, cols, slots, group, pieces,
    ids_in, probs_in, tok_in, wg_in, wu_in, wd_in, out_ref,
    ids_v, probs_v, meta, tok, wg, wu, wd, disp, comb, hid, xs, xr, yr, pr, zr, dr,
    load_sem, m_send, m_recv, pt_sem, ztok_send, ztok_recv, ctok_send, ctok_recv,
    x_send, x_recv, y_send, y_recv, p_send, p_recv, z_send, z_recv, d_send, d_recv,
):
    r = lax.axis_index("row")
    c = lax.axis_index("col")
    chips = cols // 2
    chip, core = c // 2, c % 2
    mate = 2 * chip + (1 - core)
    far = rows - 1
    partner = flip(r, far)
    count, width = tok_in.shape
    choices = ids_in.shape[0]
    per = group // 2
    chunks = chips // per
    part = group * slots
    near = far * part
    hidden = wg.shape[1]
    f_tile = math.gcd(hidden, 256)
    d_tile = math.gcd(width // pieces, 512)
    piece = width // pieces

    def remote(src, dst, send, recv, row, col):
        return pltpu.make_async_remote_copy(
            src_ref=src, dst_ref=dst, send_sem=send, recv_sem=recv,
            device_id=(row, col), device_id_type=MESH,
        )

    short = jnp.minimum(chip, chips - 1 - chip)
    side = jnp.where(2 * chip < chips, 1, -1)
    order, signs = [chip], [None]
    for p in range(1, chips):
        both = p <= 2 * short
        sign = jnp.where(both, 1 if p % 2 else -1, side)
        dist = jnp.where(both, (p + 1) // 2, p - short)
        order.append(chip + sign * dist)
        signs.append(sign)

    load_tok = pltpu.make_async_copy(tok_in, tok.at[OWN, chip, 0], load_sem.at[0])
    load_ids = pltpu.make_async_copy(ids_in, ids_v, load_sem.at[1])
    load_probs = pltpu.make_async_copy(probs_in, probs_v, load_sem.at[5])
    load_w = [
        pltpu.make_async_copy(wg_in.at[0], wg, load_sem.at[2]),
        pltpu.make_async_copy(wu_in.at[0], wu, load_sem.at[3]),
        pltpu.make_async_copy(wd_in.at[0], wd, load_sem.at[4]),
    ]
    load_tok.start()
    load_ids.start()
    load_probs.start()

    barrier = pltpu.get_barrier_semaphore()
    for d in range(1, cols):
        for row in (r, partner):
            pl.semaphore_signal(
                barrier, inc=1, device_id=(row, (c + d) % cols), device_id_type=MESH
            )
    for j in range(1, rows):
        pl.semaphore_signal(barrier, inc=1, device_id=(flip(r, j), c), device_id_type=MESH)
    pl.semaphore_wait(barrier, 2 * (cols - 1) + rows - 1)

    def hop(o, q, send, to):
        return remote(
            tok.at[o, q, 0], tok.at[o, q, 0], ztok_send.at[o, send], ztok_recv.at[o, q],
            r, 2 * ((to + chips) % chips) + core,
        )

    def onward(o, p, act):
        if p == 0:
            @pl.when(chip > 0)
            def _():
                act(hop(o, chip, 0, chip - 1))

            @pl.when(chip < chips - 1)
            def _():
                act(hop(o, chip, chips, chip + 1))
        else:
            to = chip - signs[p]

            @pl.when((to >= 0) & (to < chips))
            def _():
                act(hop(o, order[p], p, to))

    ctok = [
        [
            remote(
                tok.at[o, q, 0], tok.at[o, q, 1], ctok_send.at[o, p], ctok_recv.at[o, p], r, mate
            )
            for p, q in enumerate(order)
        ]
        for o in (OWN, PAR)
    ]
    ptok = remote(tok.at[OWN, chip, 0], tok.at[PAR, chip, 0], pt_sem.at[0], pt_sem.at[1], partner, c)

    def routing(o, d, t, slot):
        dist, other = d // 2, d % 2
        to = 2 * t + (core if other == 0 else 1 - core)
        return remote(
            meta.at[OWN, chip, 0], meta.at[o, slot, other],
            m_send.at[o, d], m_recv.at[o, slot, other], partner if o else r, to,
        )

    load_tok.wait()
    ctok[OWN][0].start()
    onward(OWN, 0, lambda copy: copy.start())
    load_ids.wait()
    load_probs.wait()
    meta[OWN, chip, 0, :choices] = ids_v[...].astype(F32)
    meta[OWN, chip, 0, choices:] = probs_v[...]
    for o in (OWN, PAR):
        for d in range(1 - o, cols):
            routing(o, d, (chip + d // 2) % chips, chip).start()
    ptok.start()
    for copy in load_w:
        copy.start()
    earlier = (
        lax.broadcasted_iota(jnp.int32, (count, count), 0)
        < lax.broadcasted_iota(jnp.int32, (count, count), 1)
    ).astype(BF16)
    slot_of = lax.broadcasted_iota(jnp.int32, (part, count), 0).astype(F32)
    lane_rows = 16
    row_id = lax.broadcasted_iota(jnp.int32, (lane_rows, count), 0)

    def route(o, i):
        for s in range(group):
            q = order[i * per + s // 2]
            ids = meta[o, q, s % 2, :choices].astype(jnp.int32)
            probs = meta[o, q, s % 2, choices:]
            named = jnp.zeros((lane_rows, count), F32)
            weights = []
            span = range(far) if o == OWN else [0]
            for j in span:
                expert = flip(r, j) * cols + c
                hit = (ids == expert).astype(F32)
                named = jnp.where(row_id == j, jnp.sum(hit, axis=0, keepdims=True), named)
                weights.append(jnp.sum(hit * probs, axis=0, keepdims=True))
            rank = jnp.dot(named.astype(BF16), earlier, preferred_element_type=F32)
            key = jnp.where(named > 0.5, rank + float(s * slots), -1.0)
            for j in span:
                one = (slot_of == key[j:j + 1, :]).astype(F32)
                at = pl.ds((j if o == OWN else far) * part, part)
                disp[at, s * count:(s + 1) * count] = one.astype(BF16)
                comb[i, at, s * count:(s + 1) * count] = (one * weights[j]).astype(BF16)

    x_out, y_out = {}, {}

    def arrive(o, d):
        if o == PAR and d == 0:
            ptok.wait_recv()
        else:
            hop(o, order[d], d, chip).wait_recv()
        onward(o, d, lambda copy: copy.start())
        ctok[o][d].start()

    def settle(o, i):
        for d in range(i * per, (i + 1) * per):
            for other in range(1 if o == OWN and d == 0 else 0, 2):
                routing(o, other, order[d], order[d]).wait_recv()
        route(o, i)
        for d in range(i * per, (i + 1) * per):
            ctok[o][d].wait_recv()

    def blocks(o, i, at):
        return jnp.concatenate(
            [tok[o, q, :, :, at].reshape(2 * count, d_tile) for q in order[i * per:(i + 1) * per]]
        )

    def dispatch(i):
        for d in range(i * per, (i + 1) * per):
            if d > 0:
                arrive(OWN, d)
        settle(OWN, i)

        def tile(n, _):
            at = pl.ds(pl.multiple_of(n * d_tile, d_tile), d_tile)
            res = jnp.dot(disp[:near], blocks(OWN, i, at), preferred_element_type=F32).astype(BF16)
            xr[i, 0, :, at] = res[:part]
            xs[i, :, :, at] = res[part:].reshape(far - 1, part, d_tile)
            return 0

        lax.fori_loop(0, width // d_tile, tile, 0)
        for j in range(1, far):
            copy = remote(
                xs.at[i, j - 1], xr.at[i, j], x_send.at[i, j], x_recv.at[i, j], flip(r, j), c
            )
            copy.start()
            x_out[i, j] = copy

    def dispatch_partner(i):
        settle(PAR, i)

        def tile(n, _):
            at = pl.ds(pl.multiple_of(n * d_tile, d_tile), d_tile)
            xr[i, far, :, at] = jnp.dot(
                disp[near:], blocks(PAR, i, at), preferred_element_type=F32
            ).astype(BF16)
            return 0

        lax.fori_loop(0, width // d_tile, tile, 0)

    def experts(i, lo, hi, first):
        if lo == 0:
            for j in range(1, far):
                x_out[i, j].wait()
        if first:
            for copy in load_w:
                copy.wait()
        size = (hi - lo) * part

        def up_tile(n, _):
            at = pl.ds(pl.multiple_of(n * f_tile, f_tile), f_tile)
            x = xr[i, lo:hi].reshape(size, width)
            gate = jnp.dot(x, wg[:, at], preferred_element_type=F32)
            up = jnp.dot(x, wu[:, at], preferred_element_type=F32)
            hid[:size, at] = (gate / (1.0 + jnp.exp(-gate)) * up).astype(BF16)
            return 0

        lax.fori_loop(0, hidden // f_tile, up_tile, 0)

        def down_tile(n, _):
            at = pl.ds(pl.multiple_of(n * d_tile, d_tile), d_tile)
            res = jnp.dot(hid[:size], wd[:, at], preferred_element_type=F32).astype(BF16)
            if lo == 0:
                yr[i, 0, :, at] = res[:part]
                xs[i, :, :, at] = res[part:near].reshape(far - 1, part, d_tile)
            if hi == rows:
                yr[i, far, :, at] = res[size - part:]
            return 0

        for h in range(pieces):
            at = pl.ds(h * piece, piece)
            lax.fori_loop(h * piece // d_tile, (h + 1) * piece // d_tile, down_tile, 0)
            if lo == 0:
                for j in range(1, far):
                    copy = remote(
                        xs.at[i, j - 1, :, at], yr.at[i, j, :, at],
                        y_send.at[i, j, h], y_recv.at[i, j, h], flip(r, j), c,
                    )
                    copy.start()
                    y_out[i, j, h] = copy

    def mate_copy(o, q, h):
        at = pl.ds(h * piece, piece)
        return remote(
            tok.at[o, q, 1, :, at], pr.at[o, q, :, at],
            p_send.at[o, q, h], p_recv.at[o, q, h], r, mate,
        )

    def combine(o, i):
        for d in range(i * per, (i + 1) * per):
            onward(o, d, lambda copy: copy.wait_send())
            ctok[o][d].wait_send()
            if o == OWN and d == 0:
                ptok.wait_send()
        lo, hi = (0, far) if o == OWN else (far, rows)
        for h in range(pieces):
            if o == OWN:
                for j in range(1, far):
                    y_out[i, j, h].wait()

            def tile(n, _):
                at = pl.ds(pl.multiple_of(n * d_tile, d_tile), d_tile)
                y = yr[i, lo:hi, :, at].reshape((hi - lo) * part, d_tile)
                res = lax.dot_general(
                    comb[i, lo * part:hi * part], y, (((0,), (0,)), ((), ())),
                    preferred_element_type=F32,
                ).astype(BF16)
                for p in range(per):
                    q = order[i * per + p]
                    tok[o, q, 0, :, at] = res[2 * p * count:(2 * p + 1) * count]
                    tok[o, q, 1, :, at] = res[(2 * p + 1) * count:(2 * p + 2) * count]
                return 0

            lax.fori_loop(h * piece // d_tile, (h + 1) * piece // d_tile, tile, 0)
            for d in range(i * per, (i + 1) * per):
                mate_copy(o, order[d], h).start()

    def chain(o, t, h, step):
        at = pl.ds(h * piece, piece)
        to = (chip + step + chips) % chips
        slot = jnp.where(to == t, chips, t) if step > 0 else t
        return remote(
            tok.at[o, t, 0, :, at], zr.at[o, slot, :, at],
            z_send.at[o, t, h], z_recv.at[o, slot, h], r, 2 * to + core,
        )

    def landed(o, slot, h):
        at = pl.ds(h * piece, piece)
        remote(
            tok.at[o, chip, 0, :, at], zr.at[o, slot, :, at],
            z_send.at[o, chip, h], z_recv.at[o, slot, h], r, mate,
        ).wait_recv()
        return zr[o, slot, :, at].astype(F32)

    def both_cores(o, q, h):
        at = pl.ds(h * piece, piece)
        return tok[o, q, 0, :, at].astype(F32) + pr[o, q, :, at].astype(F32)

    def reduce(o, k):
        for h in range(pieces):
            at = pl.ds(h * piece, piece)
            for step, t, edge in ((1, k, 0), (-1, chips - 1 - k, chips - 1)):
                @pl.when((t - chip) * step > 0)
                def _():
                    mate_copy(o, t, h).wait()

                    @pl.when(chip == edge)
                    def _():
                        tok[o, t, 0, :, at] = both_cores(o, t, h).astype(BF16)

                    @pl.when(chip != edge)
                    def _():
                        tok[o, t, 0, :, at] = (landed(o, t, h) + both_cores(o, t, h)).astype(BF16)

                    chain(o, t, h, step).start()

    def back(h):
        at = pl.ds(h * piece, piece)
        return remote(
            tok.at[PAR, chip, 0, :, at], dr.at[:, at], d_send.at[h], d_recv.at[h], partner, c
        )

    def home(o):
        for h in range(pieces):
            at = pl.ds(h * piece, piece)
            mate_copy(o, chip, h).wait()

            def finish(*slots_in):
                total = both_cores(o, chip, h)
                for slot in slots_in:
                    total = total + landed(o, slot, h)
                if o == PAR:
                    tok[PAR, chip, 0, :, at] = total.astype(BF16)
                    back(h).start()
                else:
                    back(h).wait_recv()
                    out_ref[:, at] = (total + dr[:, at].astype(F32)).astype(BF16)

            pl.when(chip == 0)(lambda: finish(chip))
            pl.when(chip == chips - 1)(lambda: finish(chips))
            pl.when((chip > 0) & (chip < chips - 1))(lambda: finish(chip, chips))

    edge_chip = (chip == 0) | (chip == chips - 1)
    for step in plan(chunks, per, chips):
        kind = step[0]
        if kind == "D":
            dispatch(step[1])
        elif kind == "F":
            if step[2] == "all":
                arrive(PAR, step[1])
            else:
                pl.when(edge_chip if step[2] == "end" else jnp.logical_not(edge_chip))(
                    functools.partial(arrive, PAR, step[1])
                )
        elif kind == "P":
            dispatch_partner(step[1])
        elif kind == "X":
            lo, hi = ((0, far), (0, rows), (far, rows))[step[2]]
            experts(step[1], lo, hi, step == ("X", 0, 1))
        elif kind == "C":
            combine(step[1], step[2])
        elif kind == "R":
            reduce(step[1], step[2])
        else:
            home(step[1])

    for o in (OWN, PAR):
        for d in range(1 - o, cols):
            routing(o, d, (chip + d // 2) % chips, chip).wait_send()
        for d in range(1, chips):
            for h in range(pieces):
                chain(o, order[d], h, 1).wait_send()
    for h in range(pieces):
        back(h).wait_send()


def body(tokens, expert_ids, gate_probs, w_gate, w_up, w_down):
    count, choices = expert_ids.shape
    width = tokens.shape[1]
    hidden = w_gate.shape[2]
    rows = lax.axis_size("row")
    cols = lax.axis_size("col")
    slots = 5 * count * choices // (4 * rows * cols * w_gate.shape[0])
    group = 2
    while group * slots % 16:
        group *= 2
    chips = cols // 2
    chunks = chips // (group // 2)
    part = group * slots
    any_spec = pl.BlockSpec(memory_space=pl.ANY)
    dma = pltpu.SemaphoreType.DMA
    scratch = [
        pltpu.VMEM((choices, count), jnp.int32),
        pltpu.VMEM((choices, count), F32),
        pltpu.VMEM((2, chips, 2, 2 * choices, count), F32),
        pltpu.VMEM((2, chips, 2, count, width), BF16),
        pltpu.VMEM((width, hidden), BF16),
        pltpu.VMEM((width, hidden), BF16),
        pltpu.VMEM((hidden, width), BF16),
        pltpu.VMEM((rows * part, group * count), BF16),
        pltpu.VMEM((chunks, rows * part, group * count), BF16),
        pltpu.VMEM((rows * part, hidden), BF16),
        pltpu.VMEM((chunks, rows - 2, part, width), BF16),
        pltpu.VMEM((chunks, rows, part, width), BF16),
        pltpu.VMEM((chunks, rows, part, width), BF16),
        pltpu.VMEM((2, chips, count, width), BF16),
        pltpu.VMEM((2, chips + 1, count, width), BF16),
        pltpu.VMEM((count, width), BF16),
        dma((6,)),
        dma((2, cols)), dma((2, chips, 2)),
        dma((2,)),
        dma((2, chips + 1)), dma((2, chips)),
        dma((2, chips)), dma((2, chips)),
        dma((chunks, rows)), dma((chunks, rows)),
        dma((chunks, rows, PIECES)), dma((chunks, rows, PIECES)),
        dma((2, chips, PIECES)), dma((2, chips, PIECES)),
        dma((2, chips, PIECES)), dma((2, chips + 1, PIECES)),
        dma((PIECES,)), dma((PIECES,)),
    ]
    return pl.pallas_call(
        functools.partial(moe_kernel, rows, cols, slots, group, PIECES),
        out_shape=jax.ShapeDtypeStruct((count, width), BF16),
        in_specs=[any_spec] * 6,
        out_specs=pl.BlockSpec(memory_space=pltpu.VMEM),
        scratch_shapes=scratch,
        compiler_params=pltpu.CompilerParams(
            collective_id=0, has_side_effects=True, vmem_limit_bytes=67043328
        ),
    )(expert_ids.T, gate_probs.T, tokens, w_gate, w_up, w_down)


def solution(mesh):
    in_specs = (
        P(("row", "col"), None),
        P(("row", "col"), None),
        P(("row", "col"), None),
        P(("row", "col"), None, None),
        P(("row", "col"), None, None),
        P(("row", "col"), None, None),
    )
    out_specs = P(("row", "col"), None)
    return jax.shard_map(body, mesh=mesh, in_specs=in_specs, out_specs=out_specs, check_vma=False)
```

time: 133 us -> 179 us (1.35)
  Pallas kernels: 131 us -> 177 us
    pallas_call x1, Pallas kernels: 131 us -> 177 us  [body(): pl.pallas_call(functools.partial(moe_kernel, rows, cols, slots, group, PI...]
where the time goes in v1:
time: 179 us; the launch traced here: 178 us
  Pallas kernels  177 us (99%)
  local copies, waits for them, and re-layouts  1.88 us (1%)
    pallas_call x1, Pallas kernels, body(): pl.pallas_call(functools.partial(moe_kernel, rows, cols, slots, group, PI...  177 us

profile of v1, /device:TPU:0, one launch (start us, length us, event | category | flops | bytes accessed | tf_op | source)
XLA Modules:
  0.0 178.5 jit_solution(15037519567258446950)
XLA Ops:
  0.0 176.6 %shard_map.64 = bf16[128,2048]{1,0:T(8,128)(2,1)} custom-call(s32[8,128]{1,0:T(8,128)} %bitcast.2, f32[8,128]{1,0:T(8,128)} %bitcast.3, bf16[128,2048]{1,0:T(8,128)(2,1)} %tok_in.1, bf16[1,2048,768]{2,1,0:T(8,128)(2,1)} %wg_in.1, bf16[1,2048,768]{2,1,0:T(8,128)(2,1)} %wu_in.1, bf16[1,768,2048]{2,1,0:T(8,128)(2,1)} %wd_in.1), custom_call_target="tpu_custom_call" | custom-call | tf_op jit(solution)/shard_map/pallas_call | solution.py:476
  176.6 1.9 %copy.8 = bf16[128,2048]{1,0:T(8,128)(2,1)} copy(bf16[128,2048]{1,0:T(8,128)(2,1)} %shard_map.64) | data formatting | bytes 1048576

commit v2 on v1

v2 whole, which is shorter than its diff:
```python
import functools
import math

import jax
import jax.numpy as jnp
from jax import lax
from jax.experimental import pallas as pl
from jax.experimental.pallas import tpu as pltpu
from jax.sharding import PartitionSpec as P

MESH = pl.DeviceIdType.MESH
BF16 = jnp.bfloat16
F32 = jnp.float32
PIECES = 4
HALVES = 2
OWN, PAR = 0, 1


def flip(r, j):
    out, bit = r, 1
    while bit <= j:
        if j & bit:
            out = out + bit * (1 - 2 * ((r // bit) % 2))
        bit *= 2
    return out


def staged(chips, per):
    return per == 1 and chips == 4


def plan(chips, per):
    hops = range(1, chips)
    every = range(chips // per)
    if not staged(chips, per):
        return (
            [("A", OWN, d, "all") for d in hops] + [("D", i) for i in every]
            + [step for i in every for step in (("X", i, 0), ("Y", i))]
            + [("C", i, "all") for i in every] + [("R", k) for k in hops]
            + [("H", OWN, "all")]
        )
    return [
        ("D", 0), ("S", 0), ("A", OWN, 1, "all"), ("A", OWN, 2, "mid"), ("D", 1), ("S", 1),
        ("X", 0, 0), ("X", 1, 0), ("Y", 1),
        ("A", OWN, 3, "mid"), ("A", OWN, 2, "end"), ("D", 2),
        ("A", PAR, 0, "all"), ("P", 0), ("CR", 1), ("A", OWN, 3, "end"), ("D", 3),
        ("A", PAR, 1, "mid"), ("P", 1), ("X", 2, 0), ("Y", 2), ("X", 1, 1), ("X", 0, 1),
        ("A", PAR, 2, "mid"), ("P", 2), ("X", 2, 1), ("X", 3, 0), ("Y", 3), ("Y", 0),
        ("CP", 2), ("CP", 0), ("CP", 1), ("CR", 2),
        ("H", PAR, "mid"), ("C", 0, "mid"), ("CR", 3), ("H", PAR, "end"), ("C", 0, "end"),
        ("H", OWN, "all"),
    ]


def moe_kernel(
    rows, cols, slots, group, pieces,
    ids_in, probs_in, tok_in, wg_in, wu_in, wd_in, out_ref,
    ids_v, probs_v, meta, tok, wg, wu, wd, disp, comb, hid, xs, xr, yr, pr, zr, es, pz, dr,
    load_sem, m_send, m_recv, pt_send, pt_recv, ztok_send, ztok_recv, ctok_send, ctok_recv,
    x_send, x_recv, y_send, y_recv, p_send, p_recv, z_send, z_recv,
    e_send, e_recv, q_send, q_recv, d_send, d_recv,
):
    r = lax.axis_index("row")
    c = lax.axis_index("col")
    chips = cols // 2
    chip, core = c // 2, c % 2
    mate = 2 * chip + (1 - core)
    far = rows - 1
    partner = flip(r, far)
    count, width = tok_in.shape
    choices = ids_in.shape[0]
    per = group // 2
    chunks = chips // per
    part = group * slots
    shared = staged(chips, per)
    modes = (OWN, PAR) if shared else (OWN,)
    reach = [far if shared and i < chunks - 1 else rows for i in range(chunks)]
    hidden = wg.shape[1]
    f_tile = math.gcd(hidden, 256)
    d_tile = math.gcd(width // pieces, 512)
    piece = width // pieces
    half = width // HALVES

    def remote(src, dst, send, recv, row, col):
        return pltpu.make_async_remote_copy(
            src_ref=src, dst_ref=dst, send_sem=send, recv_sem=recv,
            device_id=(row, col), device_id_type=MESH,
        )

    short = jnp.minimum(chip, chips - 1 - chip)
    side = jnp.where(2 * chip < chips, 1, -1)
    inner = 2 * (chip + side) + core
    outer = 2 * ((chip - side + chips) % chips) + core
    edge = short == 0
    order, signs = [chip], [None]
    for p in range(1, chips):
        both = p <= 2 * short
        sign = jnp.where(both, side if p % 2 else -side, side)
        dist = jnp.where(both, (p + 1) // 2, p - short)
        order.append(chip + sign * dist)
        signs.append(sign)

    def on_edge(act):
        pl.when(edge)(act)

    def on_mid(act):
        pl.when(jnp.logical_not(edge))(act)

    load_tok = pltpu.make_async_copy(tok_in, tok.at[OWN, chip, 0], load_sem.at[0])
    load_ids = pltpu.make_async_copy(ids_in, ids_v, load_sem.at[1])
    load_probs = pltpu.make_async_copy(probs_in, probs_v, load_sem.at[5])
    load_w = [
        pltpu.make_async_copy(wg_in.at[0], wg, load_sem.at[2]),
        pltpu.make_async_copy(wu_in.at[0], wu, load_sem.at[3]),
        pltpu.make_async_copy(wd_in.at[0], wd, load_sem.at[4]),
    ]
    load_tok.start()
    load_ids.start()
    load_probs.start()

    barrier = pltpu.get_barrier_semaphore()
    for d in range(1, cols):
        for row in (r, partner)[:len(modes)]:
            pl.semaphore_signal(
                barrier, inc=1, device_id=(row, (c + d) % cols), device_id_type=MESH
            )
    for j in range(1, rows):
        pl.semaphore_signal(barrier, inc=1, device_id=(flip(r, j), c), device_id_type=MESH)
    pl.semaphore_wait(barrier, len(modes) * (cols - 1) + rows - 1)

    def hop(o, q, send, to, h):
        at = pl.ds(h * half, half)
        return remote(
            tok.at[o, q, 0, :, at], tok.at[o, q, 0, :, at],
            ztok_send.at[o, send, h], ztok_recv.at[o, q, h],
            r, 2 * ((to + chips) % chips) + core,
        )

    def onward(o, p, h, act):
        if o == PAR:
            if p == 0:
                act(hop(PAR, chip, 0, chip + side, h))
        elif p == 0:
            @pl.when(chip > 0)
            def _():
                act(hop(OWN, chip, 0, chip - 1, h))

            @pl.when(chip < chips - 1)
            def _():
                act(hop(OWN, chip, chips, chip + 1, h))
        else:
            to = chip - signs[p]

            @pl.when((to >= 0) & (to < chips))
            def _():
                act(hop(OWN, order[p], p, to, h))

    def swap(o, p):
        return remote(
            tok.at[o, order[p], 0], tok.at[o, order[p], 1],
            ctok_send.at[o, p], ctok_recv.at[o, p], r, mate,
        )

    def share(h):
        at = pl.ds(h * half, half)
        return remote(
            tok.at[OWN, chip, 0, :, at], tok.at[PAR, chip, 0, :, at],
            pt_send.at[h], pt_recv.at[h], partner, c,
        )

    def routing(o, d, t, slot):
        dist, other = d // 2, d % 2
        to = 2 * t + (core if other == 0 else 1 - core)
        return remote(
            meta.at[OWN, chip, 0], meta.at[o, slot, other],
            m_send.at[o, d], m_recv.at[o, slot, other], partner if o else r, to,
        )

    load_tok.wait()
    swap(OWN, 0).start()
    for h in range(HALVES):
        onward(OWN, 0, h, lambda copy: copy.start())
    load_ids.wait()
    load_probs.wait()
    meta[OWN, chip, 0, :choices] = ids_v[...].astype(F32)
    meta[OWN, chip, 0, choices:] = probs_v[...]
    for o in modes:
        for d in range(1 - o, cols):
            routing(o, d, (chip + d // 2) % chips, chip).start()
    for copy in load_w:
        copy.start()
    earlier = (
        lax.broadcasted_iota(jnp.int32, (count, count), 0)
        < lax.broadcasted_iota(jnp.int32, (count, count), 1)
    ).astype(BF16)
    slot_of = lax.broadcasted_iota(jnp.int32, (part, count), 0).astype(F32)
    lane_rows = 16
    row_id = lax.broadcasted_iota(jnp.int32, (lane_rows, count), 0)

    def route(o, i, base, experts_of):
        for s in range(group):
            q = order[i * per + s // 2]
            ids = meta[o, q, s % 2, :choices].astype(jnp.int32)
            probs = meta[o, q, s % 2, choices:]
            named = jnp.zeros((lane_rows, count), F32)
            weights = []
            for j, expert in enumerate(experts_of):
                hit = (ids == expert).astype(F32)
                named = jnp.where(row_id == j, jnp.sum(hit, axis=0, keepdims=True), named)
                weights.append(jnp.sum(hit * probs, axis=0, keepdims=True))
            rank = jnp.dot(named.astype(BF16), earlier, preferred_element_type=F32)
            key = jnp.where(named > 0.5, rank + float(s * slots), -1.0)
            for j in range(len(experts_of)):
                one = (slot_of == key[j:j + 1, :]).astype(F32)
                at = pl.ds((base + j) * part, part)
                disp[at, s * count:(s + 1) * count] = one.astype(BF16)
                comb[i, at, s * count:(s + 1) * count] = (one * weights[j]).astype(BF16)

    x_out, y_out = {}, {}

    def arrive(o, d):
        for h in range(HALVES):
            if o == PAR and d == 0:
                share(h).wait_recv()
            else:
                hop(o, order[d], d, chip, h).wait_recv()
            onward(o, d, h, lambda copy: copy.start())
        swap(o, d).start()

    def heard(o, i):
        for d in range(i * per, (i + 1) * per):
            for other in range(1 if o == OWN and d == 0 else 0, 2):
                routing(o, other, order[d], order[d]).wait_recv()

    def blocks(o, i, at):
        return jnp.concatenate(
            [tok[o, q, :, :, at].reshape(2 * count, d_tile) for q in order[i * per:(i + 1) * per]]
        )

    def dispatch(i):
        heard(OWN, i)
        route(OWN, i, 0, [flip(r, j) * cols + c for j in range(reach[i])])
        for d in range(i * per, (i + 1) * per):
            swap(OWN, d).wait_recv()
        near = reach[i] * part

        def tile(n, _):
            at = pl.ds(pl.multiple_of(n * d_tile, d_tile), d_tile)
            res = jnp.dot(disp[:near], blocks(OWN, i, at), preferred_element_type=F32).astype(BF16)
            xr[i, 0, :, at] = res[:part]
            xs[i, :reach[i] - 1, :, at] = res[part:].reshape(reach[i] - 1, part, d_tile)
            return 0

        lax.fori_loop(0, width // d_tile, tile, 0)
        for j in range(1, reach[i]):
            copy = remote(
                xs.at[i, j - 1], xr.at[i, j], x_send.at[i, j], x_recv.at[i, j], flip(r, j), c
            )
            copy.start()
            x_out[i, j] = copy

    def lent(i):
        return remote(es.at[i], xr.at[i + 1, far], e_send.at[i], e_recv.at[i], r, outer)

    def repaid(i):
        return remote(
            yr.at[i + 1, far], yr.at[i, rows], q_send.at[i], q_recv.at[i], r, inner
        )

    def dispatch_partner(i):
        def work(lend):
            heard(PAR, i)
            mine = [r * cols + c] + ([r * cols + outer] if lend else [])
            route(PAR, i, far, mine)
            swap(PAR, i).wait_recv()

            def tile(n, _):
                at = pl.ds(pl.multiple_of(n * d_tile, d_tile), d_tile)
                res = jnp.dot(
                    disp[far * part:(far + len(mine)) * part], blocks(PAR, i, at),
                    preferred_element_type=F32,
                ).astype(BF16)
                xr[i, far, :, at] = res[:part]
                if lend:
                    es[i, :, at] = res[part:]
                return 0

            lax.fori_loop(0, width // d_tile, tile, 0)
            if lend:
                lent(i).start()

        on_mid(lambda: work(i < 2))
        on_edge(lambda: heard(PAR, i) if i else work(False))

    def experts(i, lo, hi, first):
        if lo == 0:
            for j in range(1, hi):
                x_out[i, j].wait()
        elif i:
            on_edge(lambda: lent(i - 1).wait_recv())
        if first:
            for copy in load_w:
                copy.wait()
        size = (hi - lo) * part

        def up_tile(n, _):
            at = pl.ds(pl.multiple_of(n * f_tile, f_tile), f_tile)
            x = xr[i, lo:hi].reshape(size, width)
            gate = jnp.dot(x, wg[:, at], preferred_element_type=F32)
            up = jnp.dot(x, wu[:, at], preferred_element_type=F32)
            hid[:size, at] = (gate / (1.0 + jnp.exp(-gate)) * up).astype(BF16)
            return 0

        lax.fori_loop(0, hidden // f_tile, up_tile, 0)

        def down_tile(n, _):
            at = pl.ds(pl.multiple_of(n * d_tile, d_tile), d_tile)
            res = jnp.dot(hid[:size], wd[:, at], preferred_element_type=F32).astype(BF16)
            if lo == 0:
                yr[i, 0, :, at] = res[:part]
                xs[i, :hi - 1, :, at] = res[part:].reshape(hi - 1, part, d_tile)
            else:
                yr[i, far, :, at] = res
            return 0

        lax.fori_loop(0, width // d_tile, down_tile, 0)
        if lo and i:
            on_edge(lambda: repaid(i - 1).start())

    def reply(i):
        for h in range(pieces):
            at = pl.ds(h * piece, piece)
            for j in range(1, reach[i]):
                copy = remote(
                    xs.at[i, j - 1, :, at], yr.at[i, j, :, at],
                    y_send.at[i, j, h], y_recv.at[i, j, h], flip(r, j), c,
                )
                copy.start()
                y_out[i, j, h] = copy

    def mate_copy(o, q, h):
        at = pl.ds(h * piece, piece)
        return remote(
            tok.at[o, q, 1, :, at], pr.at[o, q, :, at],
            p_send.at[o, q, h], p_recv.at[o, q, h], r, mate,
        )

    def weigh(o, i, lo, hi, h):
        def tile(n, _):
            at = pl.ds(pl.multiple_of(n * d_tile, d_tile), d_tile)
            y = yr[i, lo:hi, :, at].reshape((hi - lo) * part, d_tile)
            res = lax.dot_general(
                comb[i, lo * part:hi * part], y, (((0,), (0,)), ((), ())),
                preferred_element_type=F32,
            ).astype(BF16)
            for p in range(per):
                q = order[i * per + p]
                tok[o, q, 0, :, at] = res[2 * p * count:(2 * p + 1) * count]
                tok[o, q, 1, :, at] = res[(2 * p + 1) * count:(2 * p + 2) * count]
            return 0

        lax.fori_loop(h * piece // d_tile, (h + 1) * piece // d_tile, tile, 0)
        for d in range(i * per, (i + 1) * per):
            mate_copy(o, order[d], h).start()

    def free(o, d):
        for h in range(HALVES):
            onward(o, d, h, lambda copy: copy.wait_send())
            if shared and o == OWN and d == 0:
                share(h).wait_send()
        swap(o, d).wait_send()

    def combine(i, h):
        if h == 0:
            for d in range(i * per, (i + 1) * per):
                free(OWN, d)
        for j in range(1, reach[i]):
            y_out[i, j, h].wait()
        weigh(OWN, i, 0, reach[i], h)

    def combine_partner(i):
        def work(lend):
            free(PAR, i)
            if lend:
                repaid(i).wait_recv()
            for h in range(pieces):
                weigh(PAR, i, far, rows + 1 if lend else rows, h)

        on_mid(lambda: work(i < 2))
        if i == 0:
            on_edge(lambda: work(False))
        else:
            for h in range(pieces):
                on_mid(lambda: give(i, h))

    def both_cores(o, q, h):
        at = pl.ds(h * piece, piece)
        return tok[o, q, 0, :, at].astype(F32) + pr[o, q, :, at].astype(F32)

    def given(q, i, h, col):
        at = pl.ds(h * piece, piece)
        return remote(
            tok.at[PAR, q, 0, :, at], pz.at[:, at], d_send.at[i, h], d_recv.at[1, h], r, col
        )

    def give(i, h):
        q = order[i]
        at = pl.ds(h * piece, piece)
        mate_copy(PAR, q, h).wait()
        tok[PAR, q, 0, :, at] = both_cores(PAR, q, h).astype(BF16)
        given(q, i, h, inner if i == 1 else outer).start()

    def chain(t, h, step):
        at = pl.ds(h * piece, piece)
        to = (chip + step + chips) % chips
        slot = jnp.where((to == t) & (step > 0), chips, t)
        return remote(
            tok.at[OWN, t, 0, :, at], zr.at[slot, :, at],
            z_send.at[t, h], z_recv.at[slot, h], r, 2 * to + core,
        )

    def landed(slot, h):
        at = pl.ds(h * piece, piece)
        remote(
            tok.at[OWN, chip, 0, :, at], zr.at[slot, :, at],
            z_send.at[chip, h], z_recv.at[slot, h], r, mate,
        ).wait_recv()
        return zr[slot, :, at].astype(F32)

    def reduce(k, h, step):
        at = pl.ds(h * piece, piece)
        t = jnp.where(step > 0, k, chips - 1 - k)

        @pl.when((t - chip) * step > 0)
        def _():
            mate_copy(OWN, t, h).wait()
            fed = chip != jnp.where(step > 0, 0, chips - 1)

            @pl.when(jnp.logical_not(fed))
            def _():
                tok[OWN, t, 0, :, at] = both_cores(OWN, t, h).astype(BF16)

            @pl.when(fed)
            def _():
                tok[OWN, t, 0, :, at] = (landed(t, h) + both_cores(OWN, t, h)).astype(BF16)

            chain(t, h, step).start()

    def back(h):
        at = pl.ds(h * piece, piece)
        return remote(
            tok.at[PAR, chip, 0, :, at], dr.at[:, at], d_send.at[0, h], d_recv.at[0, h], partner, c
        )

    def home_partner(h):
        at = pl.ds(h * piece, piece)
        mate_copy(PAR, chip, h).wait()
        given(chip, 1, h, inner).wait_recv()
        total = both_cores(PAR, chip, h) + pz[:, at].astype(F32)
        tok[PAR, chip, 0, :, at] = total.astype(BF16)
        back(h).start()

    def home(h):
        at = pl.ds(h * piece, piece)
        mate_copy(OWN, chip, h).wait()

        def finish(*slots_in):
            total = both_cores(OWN, chip, h)
            if shared:
                back(h).wait_recv()
                total = total + dr[:, at].astype(F32)
            for slot in slots_in:
                total = total + landed(slot, h)
            out_ref[:, at] = total.astype(BF16)

        pl.when(chip == 0)(lambda: finish(chip))
        pl.when(chip == chips - 1)(lambda: finish(chips))
        pl.when((chip > 0) & (chip < chips - 1))(lambda: finish(chip, chips))

    def run(step):
        kind = step[0]
        where = {"mid": on_mid, "end": on_edge}.get(step[-1], lambda act: act())
        if kind == "S":
            share(step[1]).start()
        elif kind == "D":
            dispatch(step[1])
        elif kind == "A":
            where(lambda: arrive(step[1], step[2]))
        elif kind == "P":
            dispatch_partner(step[1])
        elif kind == "X":
            lo, hi = (far, rows) if step[2] else (0, reach[step[1]])
            experts(step[1], lo, hi, step == ("X", 0, 0))
        elif kind == "Y":
            reply(step[1])
        elif kind == "C":
            where(lambda: [combine(step[1], h) for h in range(pieces)] and None)
        elif kind == "CP":
            combine_partner(step[1])
        elif kind == "CR":
            for h in range(pieces):
                combine(step[1], h)
                reduce(step[1], h, side)
            for h in range(pieces):
                reduce(step[1], h, -side)
        elif kind == "R":
            for way in (side, -side):
                for h in range(pieces):
                    reduce(step[1], h, way)
        else:
            ends = home_partner if step[1] else home
            where(lambda: [ends(h) for h in range(pieces)] and None)

    for step in plan(chips, per):
        with jax.named_scope("_".join(str(s) for s in step)):
            run(step)

    for o in modes:
        for d in range(1 - o, cols):
            routing(o, d, (chip + d // 2) % chips, chip).wait_send()
    for d in range(1, chips):
        for h in range(pieces):
            chain(order[d], h, side).wait_send()
    if shared:
        heard(PAR, chunks - 1)
        for i in range(2):
            on_mid(lambda: lent(i).wait_send())
            on_edge(lambda: repaid(i).wait_send())
        for h in range(pieces):
            back(h).wait_send()
            for i in (1, 2):
                on_mid(lambda: given(order[i], i, h, inner).wait_send())


def body(tokens, expert_ids, gate_probs, w_gate, w_up, w_down):
    count, choices = expert_ids.shape
    width = tokens.shape[1]
    hidden = w_gate.shape[2]
    rows = lax.axis_size("row")
    cols = lax.axis_size("col")
    slots = 5 * count * choices // (4 * rows * cols * w_gate.shape[0])
    group = 2
    while group * slots % 16:
        group *= 2
    chips = cols // 2
    chunks = chips // (group // 2)
    part = group * slots
    any_spec = pl.BlockSpec(memory_space=pl.ANY)
    dma = pltpu.SemaphoreType.DMA
    kinds = 2 if staged(chips, group // 2) else 1
    scratch = [
        pltpu.VMEM((choices, count), jnp.int32),
        pltpu.VMEM((choices, count), F32),
        pltpu.VMEM((kinds, chips, 2, 2 * choices, count), F32),
        pltpu.VMEM((kinds, chips, 2, count, width), BF16),
        pltpu.VMEM((width, hidden), BF16),
        pltpu.VMEM((width, hidden), BF16),
        pltpu.VMEM((hidden, width), BF16),
        pltpu.VMEM(((rows + 1) * part, group * count), BF16),
        pltpu.VMEM((chunks, (rows + 1) * part, group * count), BF16),
        pltpu.VMEM((rows * part, hidden), BF16),
        pltpu.VMEM((chunks, rows - 1, part, width), BF16),
        pltpu.VMEM((chunks, rows, part, width), BF16),
        pltpu.VMEM((chunks, rows + 1, part, width), BF16),
        pltpu.VMEM((kinds, chips, count, width), BF16),
        pltpu.VMEM((chips + 1, count, width), BF16),
        pltpu.VMEM((2, part, width), BF16),
        pltpu.VMEM((count, width), BF16),
        pltpu.VMEM((count, width), BF16),
        dma((6,)),
        dma((kinds, cols)), dma((kinds, chips, 2)),
        dma((HALVES,)), dma((HALVES,)),
        dma((kinds, chips + 1, HALVES)), dma((kinds, chips, HALVES)),
        dma((kinds, chips)), dma((kinds, chips)),
        dma((chunks, rows)), dma((chunks, rows)),
        dma((chunks, rows, PIECES)), dma((chunks, rows, PIECES)),
        dma((kinds, chips, PIECES)), dma((kinds, chips, PIECES)),
        dma((chips, PIECES)), dma((chips + 1, PIECES)),
        dma((2,)), dma((2,)),
        dma((2,)), dma((2,)),
        dma((3, PIECES)), dma((2, PIECES)),
    ]
    return pl.pallas_call(
        functools.partial(moe_kernel, rows, cols, slots, group, PIECES),
        out_shape=jax.ShapeDtypeStruct((count, width), BF16),
        in_specs=[any_spec] * 6,
        out_specs=pl.BlockSpec(memory_space=pltpu.VMEM),
        scratch_shapes=scratch,
        compiler_params=pltpu.CompilerParams(
            collective_id=0, has_side_effects=True, vmem_limit_bytes=67043328
        ),
    )(expert_ids.T, gate_probs.T, tokens, w_gate, w_up, w_down)


def solution(mesh):
    in_specs = (
        P(("row", "col"), None),
        P(("row", "col"), None),
        P(("row", "col"), None),
        P(("row", "col"), None, None),
        P(("row", "col"), None, None),
        P(("row", "col"), None, None),
    )
    out_specs = P(("row", "col"), None)
    return jax.shard_map(body, mesh=mesh, in_specs=in_specs, out_specs=out_specs, check_vma=False)
```

time: 179 us -> 129 us (0.72)
  the two profiles are of different devices: /device:TPU:0 before, /device:TPU:6 now
where the time goes in v2:
time: 129 us
  Pallas kernels  127 us (98%)
  local copies, waits for them, and re-layouts  1.88 us (1%)
    pallas_call x1, Pallas kernels, body(): pl.pallas_call(functools.partial(moe_kernel, rows, cols, slots, group, PI...  127 us

profile of v2, /device:TPU:6, one launch (start us, length us, event | category | flops | bytes accessed | tf_op | source)
XLA Modules:
  0.0 129.0 jit_solution(13114539038634023818)
XLA Ops:
  0.0 127.1 %shard_map.64 = bf16[128,2048]{1,0:T(8,128)(2,1)} custom-call(s32[8,128]{1,0:T(8,128)} %bitcast.2, f32[8,128]{1,0:T(8,128)} %bitcast.3, bf16[128,2048]{1,0:T(8,128)(2,1)} %tok_in.1, bf16[1,2048,768]{2,1,0:T(8,128)(2,1)} %wg_in.1, bf16[1,2048,768]{2,1,0:T(8,128)(2,1)} %wu_in.1, bf16[1,768,2048]{2,1,0:T(8,128)(2,1)} %wd_in.1), custom_call_target="tpu_custom_call" | custom-call | tf_op jit(solution)/shard_map/pallas_call | solution.py:583
  127.1 1.9 %copy.8 = bf16[128,2048]{1,0:T(8,128)(2,1)} copy(bf16[128,2048]{1,0:T(8,128)(2,1)} %shard_map.64) | data formatting | bytes 1048576

commit v3 on v2

--- a/solution.py
+++ b/solution.py
@@ -32,33 +32,42 @@
 def plan(chips, per):
     hops = range(1, chips)
     every = range(chips // per)
+    halves = range(HALVES)
     if not staged(chips, per):
         return (
-            [("A", OWN, d, "all") for d in hops] + [("D", i) for i in every]
-            + [step for i in every for step in (("X", i, 0), ("Y", i))]
-            + [("C", i, "all") for i in every] + [("R", k) for k in hops]
-            + [("H", OWN, "all")]
-        )
-    return [
-        ("D", 0), ("S", 0), ("A", OWN, 1, "all"), ("A", OWN, 2, "mid"), ("D", 1), ("S", 1),
-        ("X", 0, 0), ("X", 1, 0), ("Y", 1),
-        ("A", OWN, 3, "mid"), ("A", OWN, 2, "end"), ("D", 2),
-        ("A", PAR, 0, "all"), ("P", 0), ("CR", 1), ("A", OWN, 3, "end"), ("D", 3),
-        ("A", PAR, 1, "mid"), ("P", 1), ("X", 2, 0), ("Y", 2), ("X", 1, 1), ("X", 0, 1),
-        ("A", PAR, 2, "mid"), ("P", 2), ("X", 2, 1), ("X", 3, 0), ("Y", 3), ("Y", 0),
-        ("CP", 2), ("CP", 0), ("CP", 1), ("CR", 2),
-        ("H", PAR, "mid"), ("C", 0, "mid"), ("CR", 3), ("H", PAR, "end"), ("C", 0, "end"),
-        ("H", OWN, "all"),
+            [("A", OWN, d, h, "all") for d in hops for h in halves]
+            + [("D", i, h) for i in every for h in halves]
+            + [step for i in every for step in (("X", i, 0, "all"), ("Y", i))]
+            + [("C", i, "all") for i in every] + [("R", k) for k in hops] + [("H", OWN, "all")]
+        )
+    steps = [("S", 0), ("S", 1), ("D", 0, 0), ("D", 0, 1)]
+    for h in halves:
+        steps += [("A", OWN, 1, h, "all"), ("A", OWN, 2, h, "mid"), ("D", 1, h)]
+    steps += [("T", 0, 0), ("T", 0, 1), ("A", PAR, 0, 0, "all"), ("A", PAR, 0, 1, "all"), ("P", 0)]
+    steps += [("X", 1, 0, "all"), ("Y", 1)]
+    for h in halves:
+        steps += [("A", OWN, 3, h, "mid"), ("A", OWN, 2, h, "end"), ("D", 2, h)]
+    steps += [("L", 0), ("X", 0, 0, "all")]
+    steps += [("D", 3, 0, "mid"), ("D", 3, 1, "mid"), ("CR", 1)]
+    for h in halves:
+        steps += [("A", OWN, 3, h, "end"), ("D", 3, h, "end")]
+    return steps + [
+        ("A", PAR, 1, 0, "mid"), ("A", PAR, 1, 1, "mid"), ("P", 1), ("L", 1),
+        ("X", 2, 0, "all"), ("Y", 2), ("X", 1, 1, "all"),
+        ("A", PAR, 2, 0, "mid"), ("A", PAR, 2, 1, "mid"), ("CP", 1), ("P", 2),
+        ("X", 2, 1, "all"), ("X", 0, 1, "all"), ("X", 3, 0, "all"), ("Y", 3), ("Y", 0),
+        ("CP", 2), ("CP", 0), ("CR", 2), ("H", PAR, "mid"), ("CR", 3),
+        ("H", PAR, "end"), ("C", 0, "all"), ("H", OWN, "all"),
     ]
 
 
 def moe_kernel(
     rows, cols, slots, group, pieces,
-    ids_in, probs_in, tok_in, wg_in, wu_in, wd_in, out_ref,
-    ids_v, probs_v, meta, tok, wg, wu, wd, disp, comb, hid, xs, xr, yr, pr, zr, es, pz, dr,
+    ids_in, probs_in, tok_in, wg_in, wu_in, wd_in, out_hbm,
+    out_ref, ids_v, probs_v, meta, tok, wg, wu, wd, disp, comb, hid, xs, xr, yr, pr, zr, es, pz, dr,
     load_sem, m_send, m_recv, pt_send, pt_recv, ztok_send, ztok_recv, ctok_send, ctok_recv,
     x_send, x_recv, y_send, y_recv, p_send, p_recv, z_send, z_recv,
-    e_send, e_recv, q_send, q_recv, d_send, d_recv,
+    e_send, e_recv, q_send, q_recv, d_send, d_recv, out_sem,
 ):
     r = lax.axis_index("row")
     c = lax.axis_index("col")
@@ -91,6 +100,7 @@
     side = jnp.where(2 * chip < chips, 1, -1)
     inner = 2 * (chip + side) + core
     outer = 2 * ((chip - side + chips) % chips) + core
+    across = 2 * ((chip + 2 * side + chips) % chips) + core
     edge = short == 0
     order, signs = [chip], [None]
     for p in range(1, chips):
@@ -126,6 +136,10 @@
             )
     for j in range(1, rows):
         pl.semaphore_signal(barrier, inc=1, device_id=(flip(r, j), c), device_id_type=MESH)
+    load_ids.wait()
+    load_probs.wait()
+    meta[OWN, chip, 0, :choices] = ids_v[...].astype(F32)
+    meta[OWN, chip, 0, choices:] = probs_v[...]
     pl.semaphore_wait(barrier, len(modes) * (cols - 1) + rows - 1)
 
     def hop(o, q, send, to, h):
@@ -155,10 +169,11 @@
             def _():
                 act(hop(OWN, order[p], p, to, h))
 
-    def swap(o, p):
-        return remote(
-            tok.at[o, order[p], 0], tok.at[o, order[p], 1],
-            ctok_send.at[o, p], ctok_recv.at[o, p], r, mate,
+    def swap(o, p, h):
+        at = pl.ds(h * half, half)
+        return remote(
+            tok.at[o, order[p], 0, :, at], tok.at[o, order[p], 1, :, at],
+            ctok_send.at[o, p, h], ctok_recv.at[o, p, h], r, mate,
         )
 
     def share(h):
@@ -176,17 +191,13 @@
             m_send.at[o, d], m_recv.at[o, slot, other], partner if o else r, to,
         )
 
-    load_tok.wait()
-    swap(OWN, 0).start()
-    for h in range(HALVES):
-        onward(OWN, 0, h, lambda copy: copy.start())
-    load_ids.wait()
-    load_probs.wait()
-    meta[OWN, chip, 0, :choices] = ids_v[...].astype(F32)
-    meta[OWN, chip, 0, choices:] = probs_v[...]
     for o in modes:
         for d in range(1 - o, cols):
             routing(o, d, (chip + d // 2) % chips, chip).start()
+    load_tok.wait()
+    for h in range(HALVES):
+        swap(OWN, 0, h).start()
+        onward(OWN, 0, h, lambda copy: copy.start())
     for copy in load_w:
         copy.start()
     earlier = (
@@ -216,16 +227,15 @@
                 disp[at, s * count:(s + 1) * count] = one.astype(BF16)
                 comb[i, at, s * count:(s + 1) * count] = (one * weights[j]).astype(BF16)
 
-    x_out, y_out = {}, {}
-
-    def arrive(o, d):
-        for h in range(HALVES):
-            if o == PAR and d == 0:
-                share(h).wait_recv()
-            else:
-                hop(o, order[d], d, chip, h).wait_recv()
-            onward(o, d, h, lambda copy: copy.start())
-        swap(o, d).start()
+    y_out = {}
+
+    def arrive(o, d, h):
+        if o == PAR and d == 0:
+            share(h).wait_recv()
+        else:
+            hop(o, order[d], d, chip, h).wait_recv()
+        onward(o, d, h, lambda copy: copy.start())
+        swap(o, d, h).start()
 
     def heard(o, i):
         for d in range(i * per, (i + 1) * per):
@@ -237,11 +247,12 @@
             [tok[o, q, :, :, at].reshape(2 * count, d_tile) for q in order[i * per:(i + 1) * per]]
         )
 
-    def dispatch(i):
-        heard(OWN, i)
-        route(OWN, i, 0, [flip(r, j) * cols + c for j in range(reach[i])])
+    def dispatch(i, h):
+        if h == 0:
+            heard(OWN, i)
+            route(OWN, i, 0, [flip(r, j) * cols + c for j in range(reach[i])])
         for d in range(i * per, (i + 1) * per):
-            swap(OWN, d).wait_recv()
+            swap(OWN, d, h).wait_recv()
         near = reach[i] * part
 
         def tile(n, _):
@@ -251,28 +262,35 @@
             xs[i, :reach[i] - 1, :, at] = res[part:].reshape(reach[i] - 1, part, d_tile)
             return 0
 
-        lax.fori_loop(0, width // d_tile, tile, 0)
+        lax.fori_loop(h * half // d_tile, (h + 1) * half // d_tile, tile, 0)
+
+    def slot_copy(i, j, h):
+        at = pl.ds(h * half, half)
+        return remote(
+            xs.at[i, j - 1, :, at], xr.at[i, j, :, at],
+            x_send.at[i, j, h], x_recv.at[i, j, h], flip(r, j), c,
+        )
+
+    def transmit(i, h):
         for j in range(1, reach[i]):
-            copy = remote(
-                xs.at[i, j - 1], xr.at[i, j], x_send.at[i, j], x_recv.at[i, j], flip(r, j), c
-            )
-            copy.start()
-            x_out[i, j] = copy
+            slot_copy(i, j, h).start()
 
     def lent(i):
         return remote(es.at[i], xr.at[i + 1, far], e_send.at[i], e_recv.at[i], r, outer)
 
     def repaid(i):
         return remote(
-            yr.at[i + 1, far], yr.at[i, rows], q_send.at[i], q_recv.at[i], r, inner
+            yr.at[i + 1, far], yr.at[0, rows + i], q_send.at[i], q_recv.at[i],
+            r, across if i else inner,
         )
 
     def dispatch_partner(i):
         def work(lend):
             heard(PAR, i)
             mine = [r * cols + c] + ([r * cols + outer] if lend else [])
-            route(PAR, i, far, mine)
-            swap(PAR, i).wait_recv()
+            route(PAR, i, far, mine + ([r * cols + across] if lend and i == 0 else []))
+            for h in range(HALVES):
+                swap(PAR, i, h).wait_recv()
 
             def tile(n, _):
                 at = pl.ds(pl.multiple_of(n * d_tile, d_tile), d_tile)
@@ -286,8 +304,6 @@
                 return 0
 
             lax.fori_loop(0, width // d_tile, tile, 0)
-            if lend:
-                lent(i).start()
 
         on_mid(lambda: work(i < 2))
         on_edge(lambda: heard(PAR, i) if i else work(False))
@@ -295,7 +311,8 @@
     def experts(i, lo, hi, first):
         if lo == 0:
             for j in range(1, hi):
-                x_out[i, j].wait()
+                for h in range(HALVES):
+                    slot_copy(i, j, h).wait()
         elif i:
             on_edge(lambda: lent(i - 1).wait_recv())
         if first:
@@ -368,7 +385,7 @@
             onward(o, d, h, lambda copy: copy.wait_send())
             if shared and o == OWN and d == 0:
                 share(h).wait_send()
-        swap(o, d).wait_send()
+            swap(o, d, h).wait_send()
 
     def combine(i, h):
         if h == 0:
@@ -379,16 +396,16 @@
         weigh(OWN, i, 0, reach[i], h)
 
     def combine_partner(i):
-        def work(lend):
+        def work(lent_out):
             free(PAR, i)
-            if lend:
-                repaid(i).wait_recv()
+            for j in range(lent_out):
+                repaid(j).wait_recv()
             for h in range(pieces):
-                weigh(PAR, i, far, rows + 1 if lend else rows, h)
-
-        on_mid(lambda: work(i < 2))
+                weigh(PAR, i, far, rows + lent_out, h)
+
+        on_mid(lambda: work(0 if i else 2))
         if i == 0:
-            on_edge(lambda: work(False))
+            on_edge(lambda: work(0))
         else:
             for h in range(pieces):
                 on_mid(lambda: give(i, h))
@@ -459,6 +476,10 @@
         total = both_cores(PAR, chip, h) + pz[:, at].astype(F32)
         tok[PAR, chip, 0, :, at] = total.astype(BF16)
         back(h).start()
+
+    def leave(h):
+        at = pl.ds(h * piece, piece)
+        return pltpu.make_async_copy(out_ref.at[:, at], out_hbm.at[:, at], out_sem.at[h])
 
     def home(h):
         at = pl.ds(h * piece, piece)
@@ -476,6 +497,7 @@
         pl.when(chip == 0)(lambda: finish(chip))
         pl.when(chip == chips - 1)(lambda: finish(chips))
         pl.when((chip > 0) & (chip < chips - 1))(lambda: finish(chip, chips))
+        leave(h).start()
 
     def run(step):
         kind = step[0]
@@ -483,14 +505,23 @@
         if kind == "S":
             share(step[1]).start()
         elif kind == "D":
-            dispatch(step[1])
+            def both():
+                dispatch(step[1], step[2])
+                if step[1] or not shared:
+                    transmit(step[1], step[2])
+
+            where(both)
+        elif kind == "T":
+            transmit(step[1], step[2])
+        elif kind == "L":
+            on_mid(lambda: lent(step[1]).start())
         elif kind == "A":
-            where(lambda: arrive(step[1], step[2]))
+            where(lambda: arrive(step[1], step[2], step[3]))
         elif kind == "P":
             dispatch_partner(step[1])
         elif kind == "X":
             lo, hi = (far, rows) if step[2] else (0, reach[step[1]])
-            experts(step[1], lo, hi, step == ("X", 0, 0))
+            where(lambda: experts(step[1], lo, hi, step == first))
         elif kind == "Y":
             reply(step[1])
         elif kind == "C":
@@ -511,25 +542,29 @@
             ends = home_partner if step[1] else home
             where(lambda: [ends(h) for h in range(pieces)] and None)
 
-    for step in plan(chips, per):
+    steps = plan(chips, per)
+    first = next(step for step in steps if step[0] == "X")
+    for step in steps:
         with jax.named_scope("_".join(str(s) for s in step)):
             run(step)
 
-    for o in modes:
-        for d in range(1 - o, cols):
-            routing(o, d, (chip + d // 2) % chips, chip).wait_send()
-    for d in range(1, chips):
+    with jax.named_scope("settle"):
+        for o in modes:
+            for d in range(1 - o, cols):
+                routing(o, d, (chip + d // 2) % chips, chip).wait_send()
         for h in range(pieces):
-            chain(order[d], h, side).wait_send()
-    if shared:
-        heard(PAR, chunks - 1)
-        for i in range(2):
-            on_mid(lambda: lent(i).wait_send())
-            on_edge(lambda: repaid(i).wait_send())
-        for h in range(pieces):
-            back(h).wait_send()
-            for i in (1, 2):
-                on_mid(lambda: given(order[i], i, h, inner).wait_send())
+            for d in range(1, chips):
+                chain(order[d], h, side).wait_send()
+            leave(h).wait()
+        if shared:
+            heard(PAR, chunks - 1)
+            for i in range(2):
+                on_mid(lambda: lent(i).wait_send())
+                on_edge(lambda: repaid(i).wait_send())
+            for h in range(pieces):
+                back(h).wait_send()
+                for i in (1, 2):
+                    on_mid(lambda: given(order[i], i, h, inner).wait_send())
 
 
 def body(tokens, expert_ids, gate_probs, w_gate, w_up, w_down):
@@ -549,6 +584,7 @@
     dma = pltpu.SemaphoreType.DMA
     kinds = 2 if staged(chips, group // 2) else 1
     scratch = [
+        pltpu.VMEM((count, width), BF16),
         pltpu.VMEM((choices, count), jnp.int32),
         pltpu.VMEM((choices, count), F32),
         pltpu.VMEM((kinds, chips, 2, 2 * choices, count), F32),
@@ -556,12 +592,12 @@
         pltpu.VMEM((width, hidden), BF16),
         pltpu.VMEM((width, hidden), BF16),
         pltpu.VMEM((hidden, width), BF16),
-        pltpu.VMEM(((rows + 1) * part, group * count), BF16),
-        pltpu.VMEM((chunks, (rows + 1) * part, group * count), BF16),
+        pltpu.VMEM(((rows + 2) * part, group * count), BF16),
+        pltpu.VMEM((chunks, (rows + 2) * part, group * count), BF16),
         pltpu.VMEM((rows * part, hidden), BF16),
         pltpu.VMEM((chunks, rows - 1, part, width), BF16),
         pltpu.VMEM((chunks, rows, part, width), BF16),
-        pltpu.VMEM((chunks, rows + 1, part, width), BF16),
+        pltpu.VMEM((chunks, rows + 2, part, width), BF16),
         pltpu.VMEM((kinds, chips, count, width), BF16),
         pltpu.VMEM((chips + 1, count, width), BF16),
         pltpu.VMEM((2, part, width), BF16),
@@ -571,20 +607,20 @@
         dma((kinds, cols)), dma((kinds, chips, 2)),
         dma((HALVES,)), dma((HALVES,)),
         dma((kinds, chips + 1, HALVES)), dma((kinds, chips, HALVES)),
-        dma((kinds, chips)), dma((kinds, chips)),
-        dma((chunks, rows)), dma((chunks, rows)),
+        dma((kinds, chips, HALVES)), dma((kinds, chips, HALVES)),
+        dma((chunks, rows, HALVES)), dma((chunks, rows, HALVES)),
         dma((chunks, rows, PIECES)), dma((chunks, rows, PIECES)),
         dma((kinds, chips, PIECES)), dma((kinds, chips, PIECES)),
         dma((chips, PIECES)), dma((chips + 1, PIECES)),
         dma((2,)), dma((2,)),
         dma((2,)), dma((2,)),
-        dma((3, PIECES)), dma((2, PIECES)),
+        dma((3, PIECES)), dma((2, PIECES)), dma((PIECES,)),
     ]
     return pl.pallas_call(
         functools.partial(moe_kernel, rows, cols, slots, group, PIECES),
         out_shape=jax.ShapeDtypeStruct((count, width), BF16),
         in_specs=[any_spec] * 6,
-        out_specs=pl.BlockSpec(memory_space=pltpu.VMEM),
+        out_specs=pl.BlockSpec(memory_space=pl.ANY),
         scratch_shapes=scratch,
         compiler_params=pltpu.CompilerParams(
             collective_id=0, has_side_effects=True, vmem_limit_bytes=67043328

time: 129 us -> 116 us (0.90)
  the two profiles are of different devices: /device:TPU:6 before, /device:TPU:0 now
where the time goes in v3:
time: 116 us
  Pallas kernels  114 us (98%)
  local copies, waits for them, and re-layouts  1.88 us (2%)
    pallas_call x1, Pallas kernels, body(): pl.pallas_call(functools.partial(moe_kernel, rows, cols, slots, group, PI...  114 us

profile of v3, /device:TPU:0, one launch (start us, length us, event | category | flops | bytes accessed | tf_op | source)
XLA Modules:
  0.0 116.2 jit_solution(8792694613029964993)
XLA Ops:
  0.0 114.3 %shard_map.64 = bf16[128,2048]{1,0:T(8,128)(2,1)} custom-call(s32[8,128]{1,0:T(8,128)} %bitcast.2, f32[8,128]{1,0:T(8,128)} %bitcast.3, bf16[128,2048]{1,0:T(8,128)(2,1)} %tok_in.1, bf16[1,2048,768]{2,1,0:T(8,128)(2,1)} %wg_in.1, bf16[1,2048,768]{2,1,0:T(8,128)(2,1)} %wu_in.1, bf16[1,768,2048]{2,1,0:T(8,128)(2,1)} %wd_in.1), custom_call_target="tpu_custom_call" | custom-call | tf_op jit(solution)/shard_map/pallas_call | solution.py:619
  114.3 1.9 %copy.8 = bf16[128,2048]{1,0:T(8,128)(2,1)} copy(bf16[128,2048]{1,0:T(8,128)(2,1)} %shard_map.64) | data formatting | bytes 1048576

commit v4 on v3

--- a/solution.py
+++ b/solution.py
@@ -40,10 +40,10 @@
             + [step for i in every for step in (("X", i, 0, "all"), ("Y", i))]
             + [("C", i, "all") for i in every] + [("R", k) for k in hops] + [("H", OWN, "all")]
         )
-    steps = [("S", 0), ("S", 1), ("D", 0, 0), ("D", 0, 1)]
+    steps = [("S",), ("D", 0, 0), ("D", 0, 1)]
     for h in halves:
         steps += [("A", OWN, 1, h, "all"), ("A", OWN, 2, h, "mid"), ("D", 1, h)]
-    steps += [("T", 0, 0), ("T", 0, 1), ("A", PAR, 0, 0, "all"), ("A", PAR, 0, 1, "all"), ("P", 0)]
+    steps += [("T", 0, 0), ("T", 0, 1), ("A", PAR, 0, 0, "all"), ("P", 0)]
     steps += [("X", 1, 0, "all"), ("Y", 1)]
     for h in halves:
         steps += [("A", OWN, 3, h, "mid"), ("A", OWN, 2, h, "end"), ("D", 2, h)]
@@ -52,9 +52,9 @@
     for h in halves:
         steps += [("A", OWN, 3, h, "end"), ("D", 3, h, "end")]
     return steps + [
-        ("A", PAR, 1, 0, "mid"), ("A", PAR, 1, 1, "mid"), ("P", 1), ("L", 1),
+        ("A", PAR, 1, 0, "mid"), ("P", 1), ("L", 1),
         ("X", 2, 0, "all"), ("Y", 2), ("X", 1, 1, "all"),
-        ("A", PAR, 2, 0, "mid"), ("A", PAR, 2, 1, "mid"), ("CP", 1), ("P", 2),
+        ("A", PAR, 2, 0, "mid"), ("CP", 1), ("P", 2),
         ("X", 2, 1, "all"), ("X", 0, 1, "all"), ("X", 3, 0, "all"), ("Y", 3), ("Y", 0),
         ("CP", 2), ("CP", 0), ("CR", 2), ("H", PAR, "mid"), ("CR", 3),
         ("H", PAR, "end"), ("C", 0, "all"), ("H", OWN, "all"),
@@ -65,9 +65,9 @@
     rows, cols, slots, group, pieces,
     ids_in, probs_in, tok_in, wg_in, wu_in, wd_in, out_hbm,
     out_ref, ids_v, probs_v, meta, tok, wg, wu, wd, disp, comb, hid, xs, xr, yr, pr, zr, es, pz, dr,
-    load_sem, m_send, m_recv, pt_send, pt_recv, ztok_send, ztok_recv, ctok_send, ctok_recv,
-    x_send, x_recv, y_send, y_recv, p_send, p_recv, z_send, z_recv,
-    e_send, e_recv, q_send, q_recv, d_send, d_recv, out_sem,
+    load_sem, m_send, m_recv, pt_send, pt_recv, ztok_send, ztok_recv, gtok_send, gtok_recv,
+    ctok_send, ctok_recv, stok_recv, x_send, x_recv, y_send, y_recv, p_send, p_recv, g_recv,
+    z_send, z_recv, e_send, e_recv, q_send, q_recv, d_send, d_recv, pz_recv, out_sem,
 ):
     r = lax.axis_index("row")
     c = lax.axis_index("col")
@@ -96,6 +96,9 @@
             device_id=(row, col), device_id_type=MESH,
         )
 
+    def taken(ref, sem):
+        pltpu.make_async_copy(ref, ref, sem).wait()
+
     short = jnp.minimum(chip, chips - 1 - chip)
     side = jnp.where(2 * chip < chips, 1, -1)
     inner = 2 * (chip + side) + core
@@ -143,12 +146,27 @@
     pl.semaphore_wait(barrier, len(modes) * (cols - 1) + rows - 1)
 
     def hop(o, q, send, to, h):
-        at = pl.ds(h * half, half)
+        at = pl.ds(h * half, half) if o == OWN else pl.ds(0, width)
         return remote(
             tok.at[o, q, 0, :, at], tok.at[o, q, 0, :, at],
-            ztok_send.at[o, send, h], ztok_recv.at[o, q, h],
+            ztok_send.at[send] if o == OWN else gtok_send.at[0],
+            ztok_recv.at[q, h] if o == OWN else gtok_recv.at[q],
             r, 2 * ((to + chips) % chips) + core,
         )
+
+    def sent(o, p):
+        q = order[p]
+        if o == PAR:
+            if p == 0:
+                taken(tok.at[PAR, q, 0], gtok_send.at[0])
+        elif p == 0:
+            pl.when(chip > 0)(lambda: taken(tok.at[OWN, q, 0], ztok_send.at[0]))
+            pl.when(chip < chips - 1)(lambda: taken(tok.at[OWN, q, 0], ztok_send.at[chips]))
+        else:
+            to = chip - signs[p]
+            pl.when((to >= 0) & (to < chips))(
+                lambda: taken(tok.at[OWN, q, 0], ztok_send.at[p])
+            )
 
     def onward(o, p, h, act):
         if o == PAR:
@@ -170,17 +188,15 @@
                 act(hop(OWN, order[p], p, to, h))
 
     def swap(o, p, h):
-        at = pl.ds(h * half, half)
+        at = pl.ds(h * half, half) if o == OWN else pl.ds(0, width)
         return remote(
             tok.at[o, order[p], 0, :, at], tok.at[o, order[p], 1, :, at],
-            ctok_send.at[o, p, h], ctok_recv.at[o, p, h], r, mate,
-        )
-
-    def share(h):
-        at = pl.ds(h * half, half)
-        return remote(
-            tok.at[OWN, chip, 0, :, at], tok.at[PAR, chip, 0, :, at],
-            pt_send.at[h], pt_recv.at[h], partner, c,
+            ctok_send.at[o, p], ctok_recv.at[p, h] if o == OWN else stok_recv.at[p], r, mate,
+        )
+
+    def share():
+        return remote(
+            tok.at[OWN, chip, 0], tok.at[PAR, chip, 0], pt_send.at[0], pt_recv.at[0], partner, c
         )
 
     def routing(o, d, t, slot):
@@ -188,7 +204,7 @@
         to = 2 * t + (core if other == 0 else 1 - core)
         return remote(
             meta.at[OWN, chip, 0], meta.at[o, slot, other],
-            m_send.at[o, d], m_recv.at[o, slot, other], partner if o else r, to,
+            m_send.at[2 if o else min(dist, 1)], m_recv.at[o, slot], partner if o else r, to,
         )
 
     for o in modes:
@@ -227,11 +243,10 @@
                 disp[at, s * count:(s + 1) * count] = one.astype(BF16)
                 comb[i, at, s * count:(s + 1) * count] = (one * weights[j]).astype(BF16)
 
-    y_out = {}
 
     def arrive(o, d, h):
         if o == PAR and d == 0:
-            share(h).wait_recv()
+            share().wait_recv()
         else:
             hop(o, order[d], d, chip, h).wait_recv()
         onward(o, d, h, lambda copy: copy.start())
@@ -239,8 +254,11 @@
 
     def heard(o, i):
         for d in range(i * per, (i + 1) * per):
-            for other in range(1 if o == OWN and d == 0 else 0, 2):
-                routing(o, other, order[d], order[d]).wait_recv()
+            home_only = o == OWN and d == 0
+            taken(
+                meta.at[o, order[d], 1] if home_only else meta.at[o, order[d]],
+                m_recv.at[o, order[d]],
+            )
 
     def blocks(o, i, at):
         return jnp.concatenate(
@@ -268,7 +286,7 @@
         at = pl.ds(h * half, half)
         return remote(
             xs.at[i, j - 1, :, at], xr.at[i, j, :, at],
-            x_send.at[i, j, h], x_recv.at[i, j, h], flip(r, j), c,
+            x_send.at[i], x_recv.at[i], flip(r, j), c,
         )
 
     def transmit(i, h):
@@ -289,8 +307,7 @@
             heard(PAR, i)
             mine = [r * cols + c] + ([r * cols + outer] if lend else [])
             route(PAR, i, far, mine + ([r * cols + across] if lend and i == 0 else []))
-            for h in range(HALVES):
-                swap(PAR, i, h).wait_recv()
+            swap(PAR, i, 0).wait_recv()
 
             def tile(n, _):
                 at = pl.ds(pl.multiple_of(n * d_tile, d_tile), d_tile)
@@ -310,9 +327,8 @@
 
     def experts(i, lo, hi, first):
         if lo == 0:
-            for j in range(1, hi):
-                for h in range(HALVES):
-                    slot_copy(i, j, h).wait()
+            taken(xs.at[i, :hi - 1], x_send.at[i])
+            taken(xr.at[i, 1:hi], x_recv.at[i])
         elif i:
             on_edge(lambda: lent(i - 1).wait_recv())
         if first:
@@ -348,18 +364,16 @@
         for h in range(pieces):
             at = pl.ds(h * piece, piece)
             for j in range(1, reach[i]):
-                copy = remote(
+                remote(
                     xs.at[i, j - 1, :, at], yr.at[i, j, :, at],
-                    y_send.at[i, j, h], y_recv.at[i, j, h], flip(r, j), c,
-                )
-                copy.start()
-                y_out[i, j, h] = copy
+                    y_send.at[i], y_recv.at[i, h], flip(r, j), c,
+                ).start()
 
     def mate_copy(o, q, h):
         at = pl.ds(h * piece, piece)
         return remote(
             tok.at[o, q, 1, :, at], pr.at[o, q, :, at],
-            p_send.at[o, q, h], p_recv.at[o, q, h], r, mate,
+            p_send.at[q if o else chips], p_recv.at[q, h] if o == OWN else g_recv.at[q], r, mate,
         )
 
     def weigh(o, i, lo, hi, h):
@@ -381,18 +395,16 @@
             mate_copy(o, order[d], h).start()
 
     def free(o, d):
-        for h in range(HALVES):
-            onward(o, d, h, lambda copy: copy.wait_send())
-            if shared and o == OWN and d == 0:
-                share(h).wait_send()
-            swap(o, d, h).wait_send()
+        sent(o, d)
+        if shared and o == OWN and d == 0:
+            share().wait_send()
+        taken(tok.at[o, order[d], 0], ctok_send.at[o, d])
 
     def combine(i, h):
         if h == 0:
             for d in range(i * per, (i + 1) * per):
                 free(OWN, d)
-        for j in range(1, reach[i]):
-            y_out[i, j, h].wait()
+        taken(yr.at[i, 1:reach[i], :, pl.ds(h * piece, piece)], y_recv.at[i, h])
         weigh(OWN, i, 0, reach[i], h)
 
     def combine_partner(i):
@@ -407,8 +419,7 @@
         if i == 0:
             on_edge(lambda: work(0))
         else:
-            for h in range(pieces):
-                on_mid(lambda: give(i, h))
+            on_mid(lambda: give(i))
 
     def both_cores(o, q, h):
         at = pl.ds(h * piece, piece)
@@ -417,15 +428,16 @@
     def given(q, i, h, col):
         at = pl.ds(h * piece, piece)
         return remote(
-            tok.at[PAR, q, 0, :, at], pz.at[:, at], d_send.at[i, h], d_recv.at[1, h], r, col
-        )
-
-    def give(i, h):
+            tok.at[PAR, q, 0, :, at], pz.at[:, at], d_send.at[i], pz_recv.at[0], r, col
+        )
+
+    def give(i):
         q = order[i]
-        at = pl.ds(h * piece, piece)
-        mate_copy(PAR, q, h).wait()
-        tok[PAR, q, 0, :, at] = both_cores(PAR, q, h).astype(BF16)
-        given(q, i, h, inner if i == 1 else outer).start()
+        taken(pr.at[PAR, q], g_recv.at[q])
+        for h in range(pieces):
+            at = pl.ds(h * piece, piece)
+            tok[PAR, q, 0, :, at] = both_cores(PAR, q, h).astype(BF16)
+            given(q, i, h, inner if i == 1 else outer).start()
 
     def chain(t, h, step):
         at = pl.ds(h * piece, piece)
@@ -433,14 +445,14 @@
         slot = jnp.where((to == t) & (step > 0), chips, t)
         return remote(
             tok.at[OWN, t, 0, :, at], zr.at[slot, :, at],
-            z_send.at[t, h], z_recv.at[slot, h], r, 2 * to + core,
+            z_send.at[0], z_recv.at[slot, h], r, 2 * to + core,
         )
 
     def landed(slot, h):
         at = pl.ds(h * piece, piece)
         remote(
             tok.at[OWN, chip, 0, :, at], zr.at[slot, :, at],
-            z_send.at[chip, h], z_recv.at[slot, h], r, mate,
+            z_send.at[0], z_recv.at[slot, h], r, mate,
         ).wait_recv()
         return zr[slot, :, at].astype(F32)
 
@@ -450,7 +462,7 @@
 
         @pl.when((t - chip) * step > 0)
         def _():
-            mate_copy(OWN, t, h).wait()
+            mate_copy(OWN, t, h).wait_recv()
             fed = chip != jnp.where(step > 0, 0, chips - 1)
 
             @pl.when(jnp.logical_not(fed))
@@ -466,24 +478,25 @@
     def back(h):
         at = pl.ds(h * piece, piece)
         return remote(
-            tok.at[PAR, chip, 0, :, at], dr.at[:, at], d_send.at[0, h], d_recv.at[0, h], partner, c
+            tok.at[PAR, chip, 0, :, at], dr.at[:, at], d_send.at[0], d_recv.at[h], partner, c
         )
 
     def home_partner(h):
         at = pl.ds(h * piece, piece)
-        mate_copy(PAR, chip, h).wait()
-        given(chip, 1, h, inner).wait_recv()
+        if h == 0:
+            taken(pr.at[PAR, chip], g_recv.at[chip])
+            taken(pz, pz_recv.at[0])
         total = both_cores(PAR, chip, h) + pz[:, at].astype(F32)
         tok[PAR, chip, 0, :, at] = total.astype(BF16)
         back(h).start()
 
     def leave(h):
         at = pl.ds(h * piece, piece)
-        return pltpu.make_async_copy(out_ref.at[:, at], out_hbm.at[:, at], out_sem.at[h])
+        return pltpu.make_async_copy(out_ref.at[:, at], out_hbm.at[:, at], out_sem.at[0])
 
     def home(h):
         at = pl.ds(h * piece, piece)
-        mate_copy(OWN, chip, h).wait()
+        mate_copy(OWN, chip, h).wait_recv()
 
         def finish(*slots_in):
             total = both_cores(OWN, chip, h)
@@ -503,7 +516,7 @@
         kind = step[0]
         where = {"mid": on_mid, "end": on_edge}.get(step[-1], lambda act: act())
         if kind == "S":
-            share(step[1]).start()
+            share().start()
         elif kind == "D":
             def both():
                 dispatch(step[1], step[2])
@@ -549,22 +562,24 @@
             run(step)
 
     with jax.named_scope("settle"):
-        for o in modes:
-            for d in range(1 - o, cols):
-                routing(o, d, (chip + d // 2) % chips, chip).wait_send()
-        for h in range(pieces):
-            for d in range(1, chips):
-                chain(order[d], h, side).wait_send()
-            leave(h).wait()
+        taken(meta.at[OWN, 0, 0], m_send.at[0])
+        taken(meta.at[OWN, :chips - 1], m_send.at[1])
+        for i in range(chunks):
+            taken(xs.at[i, :reach[i] - 1], y_send.at[i])
+        taken(pr.at[OWN], p_send.at[chips])
+        taken(zr.at[:chips - 1], z_send.at[0])
+        pltpu.make_async_copy(out_ref, out_hbm, out_sem.at[0]).wait()
         if shared:
+            taken(meta.at[PAR], m_send.at[2])
             heard(PAR, chunks - 1)
+            taken(pr.at[PAR, chip], p_send.at[chip])
+            taken(dr, d_send.at[0])
             for i in range(2):
                 on_mid(lambda: lent(i).wait_send())
                 on_edge(lambda: repaid(i).wait_send())
-            for h in range(pieces):
-                back(h).wait_send()
-                for i in (1, 2):
-                    on_mid(lambda: given(order[i], i, h, inner).wait_send())
+            for i in (1, 2):
+                on_mid(lambda: taken(pr.at[PAR, order[i]], p_send.at[order[i]]))
+                on_mid(lambda: taken(pz, d_send.at[i]))
 
 
 def body(tokens, expert_ids, gate_probs, w_gate, w_up, w_down):
@@ -604,17 +619,18 @@
         pltpu.VMEM((count, width), BF16),
         pltpu.VMEM((count, width), BF16),
         dma((6,)),
-        dma((kinds, cols)), dma((kinds, chips, 2)),
-        dma((HALVES,)), dma((HALVES,)),
-        dma((kinds, chips + 1, HALVES)), dma((kinds, chips, HALVES)),
-        dma((kinds, chips, HALVES)), dma((kinds, chips, HALVES)),
-        dma((chunks, rows, HALVES)), dma((chunks, rows, HALVES)),
-        dma((chunks, rows, PIECES)), dma((chunks, rows, PIECES)),
-        dma((kinds, chips, PIECES)), dma((kinds, chips, PIECES)),
-        dma((chips, PIECES)), dma((chips + 1, PIECES)),
+        dma((3,)), dma((kinds, chips)),
+        dma((1,)), dma((1,)),
+        dma((chips + 1,)), dma((chips, HALVES)),
+        dma((1,)), dma((chips,)),
+        dma((kinds, chips)), dma((chips, HALVES)), dma((chips,)),
+        dma((chunks,)), dma((chunks,)),
+        dma((chunks,)), dma((chunks, PIECES)),
+        dma((chips + 1,)), dma((chips, PIECES)), dma((chips,)),
+        dma((1,)), dma((chips + 1, PIECES)),
         dma((2,)), dma((2,)),
         dma((2,)), dma((2,)),
-        dma((3, PIECES)), dma((2, PIECES)), dma((PIECES,)),
+        dma((3,)), dma((PIECES,)), dma((1,)), dma((1,)),
     ]
     return pl.pallas_call(
         functools.partial(moe_kernel, rows, cols, slots, group, PIECES),

time: 116 us -> 114 us (0.983)
  Pallas kernels: 114 us -> 112 us
    pallas_call x1, Pallas kernels: 114 us -> 112 us  [body(): pl.pallas_call(functools.partial(moe_kernel, rows, cols, slots, group, PI...]
where the time goes in v4:
time: 114 us
  Pallas kernels  112 us (98%)
  local copies, waits for them, and re-layouts  1.88 us (2%)
    pallas_call x1, Pallas kernels, body(): pl.pallas_call(functools.partial(moe_kernel, rows, cols, slots, group, PI...  112 us

profile of v4, /device:TPU:0, one launch (start us, length us, event | category | flops | bytes accessed | tf_op | source)
XLA Modules:
  0.0 113.8 jit_solution(15605779410441663276)
XLA Ops:
  0.0 111.9 %shard_map.64 = bf16[128,2048]{1,0:T(8,128)(2,1)} custom-call(s32[8,128]{1,0:T(8,128)} %bitcast.2, f32[8,128]{1,0:T(8,128)} %bitcast.3, bf16[128,2048]{1,0:T(8,128)(2,1)} %tok_in.1, bf16[1,2048,768]{2,1,0:T(8,128)(2,1)} %wg_in.1, bf16[1,2048,768]{2,1,0:T(8,128)(2,1)} %wu_in.1, bf16[1,768,2048]{2,1,0:T(8,128)(2,1)} %wd_in.1), custom_call_target="tpu_custom_call" | custom-call | tf_op jit(solution)/shard_map/pallas_call | solution.py:635
  111.9 1.9 %copy.8 = bf16[128,2048]{1,0:T(8,128)(2,1)} copy(bf16[128,2048]{1,0:T(8,128)(2,1)} %shard_map.64) | data formatting | bytes 1048576

commit v5 on v4

--- a/solution.py
+++ b/solution.py
@@ -44,9 +44,9 @@
     for h in halves:
         steps += [("A", OWN, 1, h, "all"), ("A", OWN, 2, h, "mid"), ("D", 1, h)]
     steps += [("T", 0, 0), ("T", 0, 1), ("A", PAR, 0, 0, "all"), ("P", 0)]
-    steps += [("X", 1, 0, "all"), ("Y", 1)]
+    steps += [("A", OWN, 3, 0, "mid"), ("X", 1, 0, "all"), ("Y", 1), ("A", OWN, 3, 1, "mid")]
     for h in halves:
-        steps += [("A", OWN, 3, h, "mid"), ("A", OWN, 2, h, "end"), ("D", 2, h)]
+        steps += [("A", OWN, 2, h, "end"), ("D", 2, h)]
     steps += [("L", 0), ("X", 0, 0, "all")]
     steps += [("D", 3, 0, "mid"), ("D", 3, 1, "mid"), ("CR", 1)]
     for h in halves:
@@ -54,9 +54,10 @@
     return steps + [
         ("A", PAR, 1, 0, "mid"), ("P", 1), ("L", 1),
         ("X", 2, 0, "all"), ("Y", 2), ("X", 1, 1, "all"),
-        ("A", PAR, 2, 0, "mid"), ("CP", 1), ("P", 2),
-        ("X", 2, 1, "all"), ("X", 0, 1, "all"), ("X", 3, 0, "all"), ("Y", 3), ("Y", 0),
-        ("CP", 2), ("CP", 0), ("CR", 2), ("H", PAR, "mid"), ("CR", 3),
+        ("A", PAR, 2, 0, "mid"), ("CP", 1, "mid"), ("P", 2),
+        ("X", 2, 1, "all"), ("X", 3, 0, "all"), ("Y", 3), ("Y", 0), ("X", 0, 1, "mid"),
+        ("CP", 2, "mid"), ("CP", 0, "mid"), ("CR", 2), ("X", 0, 1, "end"), ("CP", 0, "end"),
+        ("H", PAR, "mid"), ("CR", 3),
         ("H", PAR, "end"), ("C", 0, "all"), ("H", OWN, "all"),
     ]
 
@@ -407,7 +408,7 @@
         taken(yr.at[i, 1:reach[i], :, pl.ds(h * piece, piece)], y_recv.at[i, h])
         weigh(OWN, i, 0, reach[i], h)
 
-    def combine_partner(i):
+    def combine_partner(i, role):
         def work(lent_out):
             free(PAR, i)
             for j in range(lent_out):
@@ -415,11 +416,13 @@
             for h in range(pieces):
                 weigh(PAR, i, far, rows + lent_out, h)
 
-        on_mid(lambda: work(0 if i else 2))
-        if i == 0:
-            on_edge(lambda: work(0))
+        if role == "end":
+            work(0)
+        elif i == 0:
+            work(2)
         else:
-            on_mid(lambda: give(i))
+            work(0)
+            give(i)
 
     def both_cores(o, q, h):
         at = pl.ds(h * piece, piece)
@@ -540,13 +543,17 @@
         elif kind == "C":
             where(lambda: [combine(step[1], h) for h in range(pieces)] and None)
         elif kind == "CP":
-            combine_partner(step[1])
+            where(lambda: combine_partner(step[1], step[-1]))
         elif kind == "CR":
-            for h in range(pieces):
-                combine(step[1], h)
-                reduce(step[1], h, side)
-            for h in range(pieces):
-                reduce(step[1], h, -side)
+            lag = 0 if step[1] == chunks - 1 else 1
+            for h in range(pieces + lag):
+                if h < pieces:
+                    combine(step[1], h)
+                if h >= lag:
+                    reduce(step[1], h - lag, side)
+                if h > lag:
+                    reduce(step[1], h - lag - 1, -side)
+            reduce(step[1], pieces - 1, -side)
         elif kind == "R":
             for way in (side, -side):
                 for h in range(pieces):

time: 114 us -> 111 us (0.974)
  Pallas kernels: 112 us -> 109 us
    pallas_call x1, Pallas kernels: 112 us -> 109 us  [body(): pl.pallas_call(functools.partial(moe_kernel, rows, cols, slots, group, PI...]
where the time goes in v5:
time: 111 us
  Pallas kernels  109 us (98%)
  local copies, waits for them, and re-layouts  1.88 us (2%)
    pallas_call x1, Pallas kernels, body(): pl.pallas_call(functools.partial(moe_kernel, rows, cols, slots, group, PI...  109 us

profile of v5, /device:TPU:0, one launch (start us, length us, event | category | flops | bytes accessed | tf_op | source)
XLA Modules:
  0.0 111.1 jit_solution(8427049742288939898)
XLA Ops:
  0.0 109.2 %shard_map.64 = bf16[128,2048]{1,0:T(8,128)(2,1)} custom-call(s32[8,128]{1,0:T(8,128)} %bitcast.2, f32[8,128]{1,0:T(8,128)} %bitcast.3, bf16[128,2048]{1,0:T(8,128)(2,1)} %tok_in.1, bf16[1,2048,768]{2,1,0:T(8,128)(2,1)} %wg_in.1, bf16[1,2048,768]{2,1,0:T(8,128)(2,1)} %wu_in.1, bf16[1,768,2048]{2,1,0:T(8,128)(2,1)} %wd_in.1), custom_call_target="tpu_custom_call" | custom-call | tf_op jit(solution)/shard_map/pallas_call | solution.py:642
  109.2 1.9 %copy.8 = bf16[128,2048]{1,0:T(8,128)(2,1)} copy(bf16[128,2048]{1,0:T(8,128)(2,1)} %shard_map.64) | data formatting | bytes 1048576

commit v6 on v5

--- a/solution.py
+++ b/solution.py
@@ -11,7 +11,8 @@
 MESH = pl.DeviceIdType.MESH
 BF16 = jnp.bfloat16
 F32 = jnp.float32
-PIECES = 4
+SHARES = (2, 2, 2, 1, 1)
+PIECES = len(SHARES)
 HALVES = 2
 OWN, PAR = 0, 1
 
@@ -54,9 +55,9 @@
     return steps + [
         ("A", PAR, 1, 0, "mid"), ("P", 1), ("L", 1),
         ("X", 2, 0, "all"), ("Y", 2), ("X", 1, 1, "all"),
-        ("A", PAR, 2, 0, "mid"), ("CP", 1, "mid"), ("P", 2),
-        ("X", 2, 1, "all"), ("X", 3, 0, "all"), ("Y", 3), ("Y", 0), ("X", 0, 1, "mid"),
-        ("CP", 2, "mid"), ("CP", 0, "mid"), ("CR", 2), ("X", 0, 1, "end"), ("CP", 0, "end"),
+        ("A", PAR, 2, 0, "mid"), ("CP", 1, "mid"), ("P", 2), ("G", 1),
+        ("X", 2, 1, "all"), ("CP", 2, "mid"), ("X", 3, 0, "all"), ("Y", 3), ("Y", 0), ("G", 2),
+        ("X", 0, 1, "mid"), ("CP", 0, "mid"), ("CR", 2), ("X", 0, 1, "end"), ("CP", 0, "end"),
         ("H", PAR, "mid"), ("CR", 3),
         ("H", PAR, "end"), ("C", 0, "all"), ("H", OWN, "all"),
     ]
@@ -87,9 +88,13 @@
     reach = [far if shared and i < chunks - 1 else rows for i in range(chunks)]
     hidden = wg.shape[1]
     f_tile = math.gcd(hidden, 256)
-    d_tile = math.gcd(width // pieces, 512)
-    piece = width // pieces
+    d_tile = math.gcd(width // HALVES, 512)
+    unit = width // sum(SHARES)
+    starts = [unit * sum(SHARES[:h]) for h in range(pieces + 1)]
     half = width // HALVES
+
+    def cut(h):
+        return pl.ds(starts[h], starts[h + 1] - starts[h])
 
     def remote(src, dst, send, recv, row, col):
         return pltpu.make_async_remote_copy(
@@ -281,7 +286,7 @@
             xs[i, :reach[i] - 1, :, at] = res[part:].reshape(reach[i] - 1, part, d_tile)
             return 0
 
-        lax.fori_loop(h * half // d_tile, (h + 1) * half // d_tile, tile, 0)
+        lax.fori_loop(h * half // d_tile, (h + 1) * half // d_tile, tile, 0, unroll=True)
 
     def slot_copy(i, j, h):
         at = pl.ds(h * half, half)
@@ -321,7 +326,7 @@
                     es[i, :, at] = res[part:]
                 return 0
 
-            lax.fori_loop(0, width // d_tile, tile, 0)
+            lax.fori_loop(0, width // d_tile, tile, 0, unroll=True)
 
         on_mid(lambda: work(i < 2))
         on_edge(lambda: heard(PAR, i) if i else work(False))
@@ -345,7 +350,7 @@
             hid[:size, at] = (gate / (1.0 + jnp.exp(-gate)) * up).astype(BF16)
             return 0
 
-        lax.fori_loop(0, hidden // f_tile, up_tile, 0)
+        lax.fori_loop(0, hidden // f_tile, up_tile, 0, unroll=True)
 
         def down_tile(n, _):
             at = pl.ds(pl.multiple_of(n * d_tile, d_tile), d_tile)
@@ -357,13 +362,13 @@
                 yr[i, far, :, at] = res
             return 0
 
-        lax.fori_loop(0, width // d_tile, down_tile, 0)
+        lax.fori_loop(0, width // d_tile, down_tile, 0, unroll=True)
         if lo and i:
             on_edge(lambda: repaid(i - 1).start())
 
     def reply(i):
         for h in range(pieces):
-            at = pl.ds(h * piece, piece)
+            at = cut(h)
             for j in range(1, reach[i]):
                 remote(
                     xs.at[i, j - 1, :, at], yr.at[i, j, :, at],
@@ -371,16 +376,18 @@
                 ).start()
 
     def mate_copy(o, q, h):
-        at = pl.ds(h * piece, piece)
+        at = cut(h)
         return remote(
             tok.at[o, q, 1, :, at], pr.at[o, q, :, at],
             p_send.at[q if o else chips], p_recv.at[q, h] if o == OWN else g_recv.at[q], r, mate,
         )
 
     def weigh(o, i, lo, hi, h):
+        c_tile = math.gcd(math.gcd(starts[h], starts[h + 1]), 512)
+
         def tile(n, _):
-            at = pl.ds(pl.multiple_of(n * d_tile, d_tile), d_tile)
-            y = yr[i, lo:hi, :, at].reshape((hi - lo) * part, d_tile)
+            at = pl.ds(pl.multiple_of(n * c_tile, c_tile), c_tile)
+            y = yr[i, lo:hi, :, at].reshape((hi - lo) * part, c_tile)
             res = lax.dot_general(
                 comb[i, lo * part:hi * part], y, (((0,), (0,)), ((), ())),
                 preferred_element_type=F32,
@@ -391,7 +398,7 @@
                 tok[o, q, 1, :, at] = res[(2 * p + 1) * count:(2 * p + 2) * count]
             return 0
 
-        lax.fori_loop(h * piece // d_tile, (h + 1) * piece // d_tile, tile, 0)
+        lax.fori_loop(starts[h] // c_tile, starts[h + 1] // c_tile, tile, 0, unroll=True)
         for d in range(i * per, (i + 1) * per):
             mate_copy(o, order[d], h).start()
 
@@ -405,7 +412,7 @@
         if h == 0:
             for d in range(i * per, (i + 1) * per):
                 free(OWN, d)
-        taken(yr.at[i, 1:reach[i], :, pl.ds(h * piece, piece)], y_recv.at[i, h])
+        taken(yr.at[i, 1:reach[i], :, cut(h)], y_recv.at[i, h])
         weigh(OWN, i, 0, reach[i], h)
 
     def combine_partner(i, role):
@@ -422,14 +429,13 @@
             work(2)
         else:
             work(0)
-            give(i)
 
     def both_cores(o, q, h):
-        at = pl.ds(h * piece, piece)
+        at = cut(h)
         return tok[o, q, 0, :, at].astype(F32) + pr[o, q, :, at].astype(F32)
 
     def given(q, i, h, col):
-        at = pl.ds(h * piece, piece)
+        at = cut(h)
         return remote(
             tok.at[PAR, q, 0, :, at], pz.at[:, at], d_send.at[i], pz_recv.at[0], r, col
         )
@@ -438,12 +444,12 @@
         q = order[i]
         taken(pr.at[PAR, q], g_recv.at[q])
         for h in range(pieces):
-            at = pl.ds(h * piece, piece)
+            at = cut(h)
             tok[PAR, q, 0, :, at] = both_cores(PAR, q, h).astype(BF16)
             given(q, i, h, inner if i == 1 else outer).start()
 
     def chain(t, h, step):
-        at = pl.ds(h * piece, piece)
+        at = cut(h)
         to = (chip + step + chips) % chips
         slot = jnp.where((to == t) & (step > 0), chips, t)
         return remote(
@@ -452,7 +458,7 @@
         )
 
     def landed(slot, h):
-        at = pl.ds(h * piece, piece)
+        at = cut(h)
         remote(
             tok.at[OWN, chip, 0, :, at], zr.at[slot, :, at],
             z_send.at[0], z_recv.at[slot, h], r, mate,
@@ -460,7 +466,7 @@
         return zr[slot, :, at].astype(F32)
 
     def reduce(k, h, step):
-        at = pl.ds(h * piece, piece)
+        at = cut(h)
         t = jnp.where(step > 0, k, chips - 1 - k)
 
         @pl.when((t - chip) * step > 0)
@@ -479,13 +485,13 @@
             chain(t, h, step).start()
 
     def back(h):
-        at = pl.ds(h * piece, piece)
+        at = cut(h)
         return remote(
             tok.at[PAR, chip, 0, :, at], dr.at[:, at], d_send.at[0], d_recv.at[h], partner, c
         )
 
     def home_partner(h):
-        at = pl.ds(h * piece, piece)
+        at = cut(h)
         if h == 0:
             taken(pr.at[PAR, chip], g_recv.at[chip])
             taken(pz, pz_recv.at[0])
@@ -494,11 +500,11 @@
         back(h).start()
 
     def leave(h):
-        at = pl.ds(h * piece, piece)
+        at = cut(h)
         return pltpu.make_async_copy(out_ref.at[:, at], out_hbm.at[:, at], out_sem.at[0])
 
     def home(h):
-        at = pl.ds(h * piece, piece)
+        at = cut(h)
         mate_copy(OWN, chip, h).wait_recv()
 
         def finish(*slots_in):
@@ -544,16 +550,24 @@
             where(lambda: [combine(step[1], h) for h in range(pieces)] and None)
         elif kind == "CP":
             where(lambda: combine_partner(step[1], step[-1]))
+        elif kind == "G":
+            on_mid(lambda: give(step[1]))
         elif kind == "CR":
-            lag = 0 if step[1] == chunks - 1 else 1
-            for h in range(pieces + lag):
-                if h < pieces:
-                    combine(step[1], h)
-                if h >= lag:
-                    reduce(step[1], h - lag, side)
-                if h > lag:
-                    reduce(step[1], h - lag - 1, -side)
-            reduce(step[1], pieces - 1, -side)
+            if step[1] < chunks - 1:
+                for h in range(pieces + 1):
+                    if h < pieces:
+                        combine(step[1], h)
+                    if h:
+                        reduce(step[1], h - 1, side)
+                for h in range(pieces):
+                    reduce(step[1], h, -side)
+            else:
+                turns = [(starts[h + 1] / unit, h, side) for h in range(pieces)]
+                turns += [(due + SHARES[h] + 1.8, h, -side) for due, h, _ in turns]
+                for _, h, way in sorted(turns, key=lambda turn: turn[:2]):
+                    if way is side:
+                        combine(step[1], h)
+                    reduce(step[1], h, way)
         elif kind == "R":
             for way in (side, -side):
                 for h in range(pieces):

time: 111 us -> 109 us (0.982)
  Pallas kernels: 109 us -> 107 us
    pallas_call x1, Pallas kernels: 109 us -> 107 us  [body(): pl.pallas_call(functools.partial(moe_kernel, rows, cols, slots, group, PI...]
where the time goes in v6:
time: 109 us
  Pallas kernels  107 us (98%)
  local copies, waits for them, and re-layouts  1.88 us (2%)
    pallas_call x1, Pallas kernels, body(): pl.pallas_call(functools.partial(moe_kernel, rows, cols, slots, group, PI...  107 us

profile of v6, /device:TPU:0, one launch (start us, length us, event | category | flops | bytes accessed | tf_op | source)
XLA Modules:
  0.0 108.7 jit_solution(2827819066902197495)
XLA Ops:
  0.0 106.8 %shard_map.64 = bf16[128,2048]{1,0:T(8,128)(2,1)} custom-call(s32[8,128]{1,0:T(8,128)} %bitcast.2, f32[8,128]{1,0:T(8,128)} %bitcast.3, bf16[128,2048]{1,0:T(8,128)(2,1)} %tok_in.1, bf16[1,2048,768]{2,1,0:T(8,128)(2,1)} %wg_in.1, bf16[1,2048,768]{2,1,0:T(8,128)(2,1)} %wu_in.1, bf16[1,768,2048]{2,1,0:T(8,128)(2,1)} %wd_in.1), custom_call_target="tpu_custom_call" | custom-call | tf_op jit(solution)/shard_map/pallas_call | solution.py:656
  106.8 1.9 %copy.8 = bf16[128,2048]{1,0:T(8,128)(2,1)} copy(bf16[128,2048]{1,0:T(8,128)(2,1)} %shard_map.64) | data formatting | bytes 1048576

commit v7 on v6

--- a/solution.py
+++ b/solution.py
@@ -49,9 +49,9 @@
     for h in halves:
         steps += [("A", OWN, 2, h, "end"), ("D", 2, h)]
     steps += [("L", 0), ("X", 0, 0, "all")]
-    steps += [("D", 3, 0, "mid"), ("D", 3, 1, "mid"), ("CR", 1)]
-    for h in halves:
-        steps += [("A", OWN, 3, h, "end"), ("D", 3, h, "end")]
+    steps += [("D", 3, 0, "mid"), ("D", 3, 1, "mid")]
+    steps += [("A", OWN, 3, 0, "end"), ("D", 3, 0, "end"), ("CR", 1)]
+    steps += [("A", OWN, 3, 1, "end"), ("D", 3, 1, "end")]
     return steps + [
         ("A", PAR, 1, 0, "mid"), ("P", 1), ("L", 1),
         ("X", 2, 0, "all"), ("Y", 2), ("X", 1, 1, "all"),

time: 109 us -> 109 us (level)
  no operation moved by 1% of the time
where the time goes in v7:
time: 109 us
  Pallas kernels  107 us (98%)
  local copies, waits for them, and re-layouts  1.88 us (2%)
    pallas_call x1, Pallas kernels, body(): pl.pallas_call(functools.partial(moe_kernel, rows, cols, slots, group, PI...  107 us

profile of v7, /device:TPU:0, one launch (start us, length us, event | category | flops | bytes accessed | tf_op | source)
XLA Modules:
  0.0 108.7 jit_solution(18005349126771521130)
XLA Ops:
  0.0 106.8 %shard_map.64 = bf16[128,2048]{1,0:T(8,128)(2,1)} custom-call(s32[8,128]{1,0:T(8,128)} %bitcast.2, f32[8,128]{1,0:T(8,128)} %bitcast.3, bf16[128,2048]{1,0:T(8,128)(2,1)} %tok_in.1, bf16[1,2048,768]{2,1,0:T(8,128)(2,1)} %wg_in.1, bf16[1,2048,768]{2,1,0:T(8,128)(2,1)} %wu_in.1, bf16[1,768,2048]{2,1,0:T(8,128)(2,1)} %wd_in.1), custom_call_target="tpu_custom_call" | custom-call | tf_op jit(solution)/shard_map/pallas_call | solution.py:656
  106.8 1.9 %copy.8 = bf16[128,2048]{1,0:T(8,128)(2,1)} copy(bf16[128,2048]{1,0:T(8,128)(2,1)} %shard_map.64) | data formatting | bytes 1048576
